TPU v7x, 128 devices: a whole 4x4x4 slice. The times are simulated.
128 devices in a mesh: row: 2 (over core), col: 64 (over z, y, x).
Axes of the slice: x: 4, y: 4, z: 4, core: 2. Of those that a mesh axis runs over, the one named last changes fastest.
Arguments:
- embeddings: bfloat16 [1024, 4096], P('col', 'row'), may hold values from -6 to 6
- slab_weight: bfloat16 [4096, 131072], P('row', 'col'), may hold values from -0.09375 to 0.09375
- target_table: bfloat16 [256, 131072], P(None, 'col'), may hold values from -6 to 6
- client_ids: int32 [1024], replicated, may hold values from 0 to 255
- client_weights: float32 [1024], replicated, may hold values from 0.1 to 1
Outputs:
- embed_grad: float32 [1024, 4096], P('col', 'row')
- slab_grad: float32 [4096, 131072], P('row', 'col')
Inputs may be any that keep to these rules, and one draw needn't show every extreme that they name: `client_ids`: table rows may repeat among clients.
All inputs are finite; a program needn't handle non-finite values.
Results may differ from a plain program's by a relative error of at most 0.0065.
Values may be sent and summed in bfloat16 or wider, within the bound.
No kernel may reach another device: no remote copies, remote signals or barrier semaphores. Data moves between devices by JAX's collectives and lax.ppermute only.
A program may use at most 128 MiB of HBM per device.

v0:
```python
import jax
import jax.numpy as jnp
from jax import lax
from jax.sharding import PartitionSpec as P


def total_of_pieces(value, axis):
    pieces = lax.all_gather(value, axis).astype(jnp.float32)
    return pieces.sum(axis=0)


def cut_along(value, dim, size):
    before, after = (value.shape[:dim], value.shape[dim + 1 :])
    return jnp.moveaxis(value.reshape(*before, size, -1, *after), dim, 0)


def summed_on_arrival(value, axis, dim):
    size = lax.axis_size(axis)
    pieces = lax.all_to_all(cut_along(value, dim, size), axis, 0, 0, tiled=True)
    return jnp.sum(pieces.astype(jnp.float32), axis=0)


def make_residual(emitted, target_table, own_ids, own_weights):
    target = jnp.take(target_table, own_ids, axis=0).astype(jnp.float32)
    return (own_weights[:, None] * (emitted - target)).astype(jnp.bfloat16)


def transpose_product(rows_block, slab_weight):
    return lax.dot_general(
        rows_block, slab_weight, (((1,), (1,)), ((), ())), preferred_element_type=jnp.float32
    )


def per_device(embeddings, slab_weight, target_table, client_ids, client_weights):
    features = lax.all_gather(embeddings, "col", axis=0, tiled=True)
    partial_value = jnp.dot(features, slab_weight, preferred_element_type=jnp.float32)
    whole_sum = total_of_pieces(partial_value.astype(jnp.bfloat16), "row").astype(jnp.float32)
    full_residual = make_residual(whole_sum, target_table, client_ids, client_weights)
    weight_grad = lax.dot_general(
        features, full_residual, (((0,), (0,)), ((), ())), preferred_element_type=jnp.float32
    )
    collected = transpose_product(full_residual, slab_weight)
    embed_grad = summed_on_arrival(collected.astype(jnp.bfloat16), "col", 0)
    return (embed_grad, weight_grad)


def solution(mesh):
    placed = (P("col", "row"), P("row", "col"), P(None, "col"), P(), P())
    return jax.shard_map(
        per_device,
        mesh=mesh,
        in_specs=placed,
        out_specs=(P("col", "row"), P("row", "col")),
        check_vma=False,
    )
```

profile of v0, /device:TPU:0, one launch (start us, length us, event | category | flops | bytes accessed | tf_op | source)
XLA Modules:
  0.0 220.2 jit_solution(1905359356213014758)
XLA Ops:
  7.2 0.0 copy-start
  7.2 0.0 all-gather.4.cloned.1.call-start
  7.2 0.7 all-gather.4.cloned.1.call-update
  7.9 0.0 all-gather.6.cloned.1.call-start
  8.0 74.0 %all-gather.4.cloned.1.call-done = bf16[1024,2048]{1,0:T(8,128)(2,1)} async-done(((bf16[16,2048]{1,0:T(8,128)(2,1)}), bf16[1024,2048]{1,0:T(8,128)(2,1)}) %all-gather.4.cloned.1.call-update) | async-done | bytes 4194320 | tf_op jit(solution)/shard_map/all_gather | solution.py:35
  82.0 13.8 %convolution_convert_fusion.1 = bf16[1024,2048]{1,0:T(8,128)(2,1)} fusion(bf16[1024,2048]{1,0:T(8,128)(2,1)} %all-gather.4.cloned.1.call-done, bf16[2048,2048]{1,0:T(8,128)(2,1)} %param.6), kind=kOutput, calls=%fused_computation.6 | convolution fusion | flops 8592031744 | bytes 16777216 | tf_op jit(solution)/shard_map/dot_general | solution.py:36
  95.8 0.0 all-gather.6.cloned.1.call-update
  95.8 0.7 copy-done.4
  96.5 0.0 copy-done
  96.5 6.0 %gather_fusion = bf16[1024,2048]{1,0:T(8,128)(2,1)} fusion(bf16[256,2048]{1,0:T(8,128)(2,1)S(1)} %copy-done, s32[1024]{0:T(1024)S(1)} %fusion), kind=kCustom, calls=%fused_computation | custom fusion | bytes 8392704 | tf_op jit(solution)/shard_map/jit(_take)/gather | solution.py:24
  102.5 13.3 %all-gather.6.cloned.1.call-done = bf16[2048,2048]{1,0:T(8,128)(2,1)} async-done(((bf16[1024,2048]{1,0:T(8,128)(2,1)}), bf16[2048,2048]{1,0:T(8,128)(2,1)}) %all-gather.6.cloned.1.call-update) | async-done | bytes 8388624 | tf_op jit(solution)/shard_map/all_gather | solution.py:8
  115.9 10.0 %convert_reduce_fusion = f32[1024,2048]{1,0:T(8,128)} fusion(bf16[2,1024,2048]{2,1,0:T(8,128)(2,1)} %bitcast.11), kind=kLoop, calls=%fused_computation.1 | loop fusion | flops 6291456 | bytes 16777216 | tf_op jit(solution)/shard_map/reduce_sum | solution.py:9
  125.9 0.0 copy-done.2
  125.9 0.0 copy-done.5
  125.9 4.4 %multiply_convert_fusion = bf16[1024,2048]{1,0:T(8,128)(2,1)S(1)} fusion(f32[1024,2048]{1,0:T(8,128)} %convert_reduce_fusion, bf16[1024,2048]{1,0:T(8,128)(2,1)S(1)} %copy-done.2, f32[1024]{0:T(1024)S(1)} %copy-done.5, pred[1024]{0:T(1024)(128)(4,1)S(1)} %compare_and_fusion), kind=kLoop, calls=%fused_computation.4 | loop fusion | flops 10485760 | bytes 16782336 | tf_op jit(solution)/shard_map/convert_element_type | solution.py:25
  130.3 0.0 copy-start.3
  130.3 14.2 %convolution_convert_fusion = bf16[1024,2048]{1,0:T(8,128)(2,1)} fusion(bf16[1024,2048]{1,0:T(8,128)(2,1)S(1)} %multiply_convert_fusion, bf16[2048,2048]{1,0:T(8,128)(2,1)} %param.6), kind=kOutput, calls=%fused_computation.5 | convolution fusion | flops 8592031744 | bytes 16777216 | tf_op jit(solution)/shard_map/dot_general | solution.py:29
  144.5 0.0 copy-done.3
  144.5 10.7 %all-to-all-start = ((bf16[64,16,2048]{2,1,0:T(8,128)(2,1)}), bf16[64,16,2048]{2,1,0:T(8,128)(2,1)}, u32[]{:S(2)}, u32[]{:S(2)}) async-start(bf16[64,16,2048]{2,1,0:T(8,128)(2,1)} %bitcast.12), calls=%async_computation | async-start | bytes 8388608 | tf_op jit(solution)/shard_map/all_to_all | solution.py:19
  155.2 15.3 %convolution_bitcast_fusion = f32[2048,2048]{0,1:T(8,128)} fusion(bf16[1024,2048]{1,0:T(8,128)(2,1)} %copy-done.3, bf16[1024,2048]{1,0:T(8,128)(2,1)} %all-gather.4.cloned.1.call-done), kind=kOutput, calls=%fused_computation.2 | convolution fusion | flops 8589934592 | bytes 25165824 | tf_op jit(solution)/shard_map/dot_general | solution.py:39
  170.5 17.7 %copy.7 = f32[2048,2048]{1,0:T(8,128)} copy(f32[2048,2048]{0,1:T(8,128)} %convolution_bitcast_fusion) | data formatting | bytes 33554432
  188.1 21.7 %all-to-all-done = bf16[64,16,2048]{2,1,0:T(8,128)(2,1)} async-done(((bf16[64,16,2048]{2,1,0:T(8,128)(2,1)}), bf16[64,16,2048]{2,1,0:T(8,128)(2,1)}, u32[]{:S(2)}, u32[]{:S(2)}) %all-to-all-start) | async-done | bytes 4194336 | tf_op jit(solution)/shard_map/all_to_all | solution.py:19
  209.9 3.5 %convert_reduce_fusion.1 = f32[16,2048]{1,0:T(8,128)} fusion(bf16[64,16,2048]{2,1,0:T(8,128)(2,1)} %all-to-all-done), kind=kLoop, calls=%fused_computation.3 | loop fusion | flops 4161536 | bytes 4325376 | tf_op jit(solution)/shard_map/reduce_sum | solution.py:20
  213.4 0.0 copy-done.1
  (6 shorter events, 0.0 us)
Async XLA Ops:
  7.2 89.3 %copy-start = (bf16[256,2048]{1,0:T(8,128)(2,1)S(1)}, bf16[256,2048]{1,0:T(8,128)(2,1)}, u32[]{:S(2)}) copy-start(bf16[256,2048]{1,0:T(8,128)(2,1)} %param.7) | copy-start | bytes 3145732
  7.2 74.8 %all-gather.4.cloned.1.call-start = ((), (), s32[]{:S(2)}) async-start(), calls=%async_computation.1 | async-start | bytes 4259840 | tf_op jit(solution)/shard_map/all_gather | solution.py:35
  7.9 107.9 %all-gather.6.cloned.1.call-start = ((), (), s32[]{:S(2)}) async-start(), calls=%async_computation.2 | async-start | bytes 12582912 | tf_op jit(solution)/shard_map/all_gather | solution.py:8
  95.8 0.7 copy-start.4
  115.8 10.0 %copy-start.2 = (bf16[1024,2048]{1,0:T(8,128)(2,1)S(1)}, bf16[1024,2048]{1,0:T(8,128)(2,1)}, u32[]{:S(2)}) copy-start(bf16[1024,2048]{1,0:T(8,128)(2,1)} %gather_fusion) | copy-start | bytes 12582916
  115.8 10.0 %copy-start.5 = (f32[1024]{0:T(1024)S(1)}, f32[1024]{0:T(1024)}, u32[]{:S(2)}) copy-start(f32[1024]{0:T(1024)} %param.9) | copy-start | bytes 12292
  130.3 14.2 %copy-start.3 = (bf16[1024,2048]{1,0:T(8,128)(2,1)}, bf16[1024,2048]{1,0:T(8,128)(2,1)S(1)}, u32[]{:S(2)}) copy-start(bf16[1024,2048]{1,0:T(8,128)(2,1)S(1)} %multiply_convert_fusion) | copy-start | bytes 12582916
  144.5 65.4 %all-to-all-start = ((bf16[64,16,2048]{2,1,0:T(8,128)(2,1)}), bf16[64,16,2048]{2,1,0:T(8,128)(2,1)}, u32[]{:S(2)}, u32[]{:S(2)}) async-start(bf16[64,16,2048]{2,1,0:T(8,128)(2,1)} %bitcast.12), calls=%async_computation | async-start | bytes 8388608 | tf_op jit(solution)/shard_map/all_to_all | solution.py:19
  170.5 42.9 %copy-start.1 = (bf16[256,2048]{1,0:T(8,128)(2,1)S(1)}, bf16[256,2048]{1,0:T(8,128)(2,1)}, u32[]{:S(2)}) copy-start(bf16[256,2048]{1,0:T(8,128)(2,1)} %param.7) | copy-start | bytes 3145732
Sparse Core Ops, SparseCore 0:
  10.9 71.0 all-gather.3
  95.9 19.8 all-gather.5
where the time goes:
time: 221 us; the launch traced here: 220 us
  waiting for transfers between devices  110 us (50%)
  matrix products  43.3 us (20%)
  local copies, waits for them, and re-layouts  24.4 us (11%)
  other arithmetic  17.9 us (8%)
  between operations  14.1 us (6%)
  starting transfers between devices  10.7 us (5%)
    all_gather x1, waiting for transfers between devices, per_device(): features = lax.all_gather(embeddings, 'col', axis=0, tiled=True)  74 us
    all_to_all x1, waiting for transfers between devices, summed_on_arrival(): pieces = lax.all_to_all(cut_along(value, dim, size), axis, 0, 0, tiled=True)  21.7 us
    unnamed x13, local copies, waits for them, and re-layouts  18.4 us
    dot_general x1, matrix products, per_device(): lax.dot_general(features, full_residual, (((0,), (0,)), ((), ())), prefer...  15.3 us
    dot_general x1, matrix products, transpose_product(): lax.dot_general(rows_block, slab_weight, (((1,), (1,)), ((), ())), prefer...  14.2 us
    dot_general x1, matrix products, per_device(): jnp.dot(features, slab_weight, preferred_element_type=jnp.float32)  13.8 us
    all_gather x1, waiting for transfers between devices, total_of_pieces(): pieces = lax.all_gather(value, axis).astype(jnp.float32)  13.3 us
    all_to_all x1, starting transfers between devices, summed_on_arrival(): pieces = lax.all_to_all(cut_along(value, dim, size), axis, 0, 0, tiled=True)  10.7 us
  transfers between devices with their start and end apart: 3, of which 3 were waited for; matrix products, arithmetic and copies ran while one was open for 18% of the time, Pallas kernels for 0%

commit v1 on v0

v1 whole, which is shorter than its diff:
```python
import jax
import jax.numpy as jnp
from jax import lax
from jax.experimental import pallas as pl
from jax.experimental.pallas import tpu as pltpu
from jax.sharding import PartitionSpec as P

STRIDE = {"x": 1, "y": 4, "z": 16}
ORDER = (("x", "y", "z"), ("x", "z", "y"))


def hop(value, phase, offset):
    pairs = []
    for core in range(2):
        stride = STRIDE[ORDER[core][phase]]
        for chip in range(64):
            at = (chip // stride) % 4
            to = chip + ((at + offset) % 4 - at) * stride
            pairs.append((core * 64 + chip, core * 64 + to))
    return lax.ppermute(value, ("row", "col"), pairs)


def fetch(value, phase, offset):
    return hop(value, phase, -offset)


def across(value):
    return lax.ppermute(value, "row", [(0, 1), (1, 0)])


def row_order():
    chip = lax.axis_index("col")
    core = lax.axis_index("row")
    ks = lax.broadcasted_iota(jnp.int32, (64,), 0)
    k3, k2, k1 = ks // 16, (ks // 4) % 4, ks % 4
    dz = jnp.where(core == 0, k3, k2)
    dy = jnp.where(core == 0, k2, k3)
    z, y, x = chip // 16, (chip // 4) % 4, chip % 4
    return ((z + dz) % 4) * 16 + ((y + dy) % 4) * 4 + (x + k1) % 4


def residual_kernel(own_ref, r0_ref, r1_ref, r2_ref, r3_ref, out_ref):
    step = own_ref.shape[0] // 4
    for q, ref in enumerate((r0_ref, r1_ref, r2_ref, r3_ref)):
        span = slice(q * step, (q + 1) * step)
        both = own_ref[span, :].astype(jnp.float32) + ref[0].astype(jnp.float32)
        out_ref[span, :] = both.astype(jnp.bfloat16)


def residual_plane(k, own, others):
    rows, width = own.shape
    cols = 1024
    theirs = pl.BlockSpec((1, rows // 4, cols), lambda j: (k, 0, j))
    return pl.pallas_call(
        residual_kernel,
        grid=(width // cols,),
        in_specs=[pl.BlockSpec((rows, cols), lambda j: (0, j)), theirs, theirs, theirs, theirs],
        out_specs=pl.BlockSpec((rows, cols), lambda j: (0, j)),
        out_shape=jax.ShapeDtypeStruct((rows, width), jnp.bfloat16),
        compiler_params=pltpu.CompilerParams(vmem_limit_bytes=8 * 2**20),
        cost_estimate=pl.CostEstimate(flops=rows * width * 64, bytes_accessed=3 * 2**20, transcendentals=0),
        name="residual",
    )(own, *others)


def slab_kernel(e0, e1, e2, e3, r0, r1, r2, r3, out_ref, e_all, r_all):
    step = e0.shape[0]

    @pl.when(pl.program_id(0) == 0)
    def _():
        for q, ref in enumerate((r0, r1, r2, r3)):
            r_all[q * step : (q + 1) * step, :] = ref[...]

    for q, ref in enumerate((e0, e1, e2, e3)):
        e_all[q * step : (q + 1) * step, :] = ref[...]
    out_ref[...] = lax.dot_general(
        e_all[...], r_all[...], (((0,), (0,)), ((), ())), preferred_element_type=jnp.float32
    )


def slab_product(planes, residuals):
    rows, hidden = planes[0].shape
    width = residuals[0].shape[1]
    block = 256
    return pl.pallas_call(
        slab_kernel,
        grid=(hidden // block,),
        in_specs=[pl.BlockSpec((rows, block), lambda i: (0, i))] * 4 + [pl.BlockSpec((rows, width), lambda i: (0, 0))] * 4,
        out_specs=pl.BlockSpec((block, width), lambda i: (i, 0)),
        out_shape=jax.ShapeDtypeStruct((hidden, width), jnp.float32),
        scratch_shapes=[pltpu.VMEM((4 * rows, block), jnp.bfloat16), pltpu.VMEM((4 * rows, width), jnp.bfloat16)],
        compiler_params=pltpu.CompilerParams(dimension_semantics=("arbitrary",), vmem_limit_bytes=40 * 2**20),
        cost_estimate=pl.CostEstimate(
            flops=8 * rows * hidden * width, bytes_accessed=24 * 2**20, transcendentals=0
        ),
        name="slab_grad",
    )(*planes, *residuals)


def per_device(embeddings, slab_weight, target_table, client_ids, client_weights):
    value = embeddings
    for phase in range(2):
        value = jnp.stack([value, *(fetch(value, phase, k) for k in (1, 2, 3))])
        value = value.reshape(-1, value.shape[-1])
    rows = value.shape[0]
    planes = {0: value}
    for k in (1, 3):
        planes[k] = fetch(value, 2, k)
    upper = fetch(planes[1][: rows // 2], 2, 1)
    lower = fetch(planes[3][rows // 2 :], 2, 3)
    planes[2] = jnp.concatenate([upper, lower])
    block = row_order()
    ids = client_ids.reshape(64, 16)[block].reshape(-1)
    weights = client_weights.reshape(64, 16)[block].reshape(4, rows)
    picks = (ids[:, None] == lax.broadcasted_iota(jnp.int32, (1, target_table.shape[0]), 1)).astype(jnp.bfloat16)
    target = jnp.dot(picks, target_table, preferred_element_type=jnp.float32).astype(jnp.bfloat16)
    target, weights = lax.optimization_barrier((target, weights))
    target = target.reshape(4, rows, -1)
    partial, other = {}, {}
    for k in (0, 1, 3, 2):
        part = jnp.dot(planes[k], slab_weight, preferred_element_type=jnp.float32)
        part = weights[k][:, None] * (part - 0.5 * target[k].astype(jnp.float32))
        partial[k] = part.astype(jnp.bfloat16)
        other[k] = across(partial[k])
    others = [other[k].reshape(4, rows // 4, -1) for k in range(4)]
    residual, sent = {}, {}
    for k in (2, 1, 3, 0):
        residual[k] = residual_plane(k, partial[k], others)
        part = lax.dot_general(residual[k], slab_weight, (((1,), (1,)), ((), ())), preferred_element_type=jnp.float32)
        part = part.astype(jnp.bfloat16) if k else lax.optimization_barrier(part)
        sent[k] = hop(part, 2, k) if k else part
    slab_grad = slab_product([planes[k] for k in range(4)], [residual[k] for k in range(4)])
    total = sum(sent[k].astype(jnp.float32) for k in range(4))
    for phase in (1, 0):
        cut = total.reshape(4, -1, total.shape[-1])
        total = cut[0] + sum(hop(cut[k].astype(jnp.bfloat16), phase, k).astype(jnp.float32) for k in (1, 2, 3))
    return total, slab_grad


def solution(mesh):
    placed = (P("col", "row"), P("row", "col"), P(None, "col"), P(), P())
    return jax.shard_map(
        per_device,
        mesh=mesh,
        in_specs=placed,
        out_specs=(P("col", "row"), P("row", "col")),
        check_vma=False,
    )
```

time: 221 us -> 126 us (0.57)
  waiting for transfers between devices: 110 us -> 43.9 us
  local copies, waits for them, and re-layouts: 24.4 us -> 3.51 us
  starting transfers between devices: 10.7 us -> 30.5 us
  Pallas kernels: 0 us -> 15.4 us
  other arithmetic: 17.9 us -> 2.53 us
  matrix products: 43.3 us -> 29.1 us
  between operations: 14.1 us -> 0.95 us
    all_gather x2 -> x0, waiting for transfers between devices: 87.4 us -> none  [the longest x1 74 us: per_device(): features = lax.all_gather(embeddings, 'col', axis=0, tiled=True)]
    ppermute x0 -> x23, waiting for transfers between devices: none -> 43.9 us  [the longest x19 41.3 us: hop(): return lax.ppermute(value, ('row', 'col'), pairs)]
    ppermute x0 -> x23, starting transfers between devices: none -> 30.5 us  [the longest x19 29.5 us: hop(): return lax.ppermute(value, ('row', 'col'), pairs)]
    all_to_all x1 -> x0, waiting for transfers between devices: 21.7 us -> none  [summed_on_arrival(): pieces = lax.all_to_all(cut_along(value, dim, size), axis, 0, 0, tiled=True)]
    unnamed x13 -> x11, local copies, waits for them, and re-layouts: 18.4 us -> 0.07 us
    pallas_call x0 -> x5, Pallas kernels: none -> 15.4 us  [the longest x1 13.3 us: slab_product(): pl.pallas_call(slab_kernel, grid=(hidden // block,), in_specs=[pl.BlockSp...]
    dot_general x3 -> x9, matrix products: 43.3 us -> 29.1 us  [the longest x4 14.4 us: per_device(): part = jnp.dot(planes[k], slab_weight, preferred_element_type=jnp.float32)]
    reduce_sum x2 -> x0, other arithmetic: 13.5 us -> none  [the longest x1 10 us: total_of_pieces(): return pieces.sum(axis=0)]
  transfers between devices with their start and end apart: 3 -> 23, of which waited for: 3 -> 14; matrix products, arithmetic and copies ran while one was open for 18% -> 24% of each run, Pallas kernels for 0% -> 11%
where the time goes in v1:
time: 126 us
  waiting for transfers between devices  43.9 us (35%)
  starting transfers between devices  30.5 us (24%)
  matrix products  29.1 us (23%)
  Pallas kernels  15.4 us (12%)
  local copies, waits for them, and re-layouts  3.51 us (3%)
  other arithmetic  2.53 us (2%)
    ppermute x19, waiting for transfers between devices, hop(): return lax.ppermute(value, ('row', 'col'), pairs)  41.3 us
    ppermute x19, starting transfers between devices, hop(): return lax.ppermute(value, ('row', 'col'), pairs)  29.5 us
    dot_general x4, matrix products, per_device(): part = jnp.dot(planes[k], slab_weight, preferred_element_type=jnp.float32)  14.4 us
    pallas_call x1, Pallas kernels, slab_product(): pl.pallas_call(slab_kernel, grid=(hidden // block,), in_specs=[pl.BlockSp...  13.3 us
    dot_general x4, matrix products, per_device(): lax.dot_general(residual[k], slab_weight, (((1,), (1,)), ((), ())), prefe...  11.4 us
    dot_general x1, matrix products, per_device(): jnp.dot(picks, target_table, preferred_element_type=jnp.float32)  3.31 us
    ppermute x4, waiting for transfers between devices, across(): return lax.ppermute(value, 'row', [(0, 1), (1, 0)])  2.62 us
  transfers between devices with their start and end apart: 23, of which 14 were waited for; matrix products, arithmetic and copies ran while one was open for 24% of the time, Pallas kernels for 11%

profile of v1, /device:TPU:0, one launch (start us, length us, event | category | flops | bytes accessed | tf_op | source)
XLA Modules:
  0.0 125.9 jit_solution(3302494857865351261)
XLA Ops:
  0.6 2.9 %collective-permute-start = (bf16[16,2048]{1,0:T(8,128)(2,1)}, bf16[16,2048]{1,0:T(8,128)(2,1)S(1)}, u32[]{:S(2)}, u32[]{:S(2)}) collective-permute-start(bf16[16,2048]{1,0:T(8,128)(2,1)} %param.5), channel_id=1, source_target_pairs={{0,3},{1,0},{2,1},{3,2},{4,7},{5,4},{6,5},{7,6},{8,11},{9,8},{10,9... | collective-permute-start | bytes 196616 | tf_op jit(solution)/shard_map/ppermute | solution.py:20
  6.1 3.4 %collective-permute-done.1 = bf16[16,2048]{1,0:T(8,128)(2,1)S(1)} collective-permute-done((bf16[16,2048]{1,0:T(8,128)(2,1)}, bf16[16,2048]{1,0:T(8,128)(2,1)S(1)}, u32[]{:S(2)}, u32[]{:S(2)}) %collective-permute-start.1) | collective-permute-done | bytes 65568 | tf_op jit(solution)/shard_map/ppermute | solution.py:20
  19.2 3.7 %collective-permute-done.4 = bf16[64,2048]{1,0:T(8,128)(2,1)S(1)} collective-permute-done((bf16[64,2048]{1,0:T(8,128)(2,1)S(1)}, bf16[64,2048]{1,0:T(8,128)(2,1)S(1)}, u32[]{:S(2)}, u32[]{:S(2)}) %collective-permute-start.4) | collective-permute-done | bytes 262176 | tf_op jit(solution)/shard_map/ppermute | solution.py:20
  23.0 4.1 %collective-permute-start.7 = (bf16[256,2048]{1,0:T(8,128)(2,1)S(1)}, bf16[256,2048]{1,0:T(8,128)(2,1)S(1)}, u32[]{:S(2)}, u32[]{:S(2)}) collective-permute-start(bf16[256,2048]{1,0:T(8,128)(2,1)S(1)} %bitcast.53), channel_id=1, source_target_pairs={{0,48},{1,49},{2,50},{3,51},{4,52},{5,53},{6,54},{7,55},{8,56},{9,... | collective-permute-start | bytes 3145736 | tf_op jit(solution)/shard_map/ppermute | solution.py:20
  27.1 3.3 %convolution_convert_fusion = bf16[1024,2048]{1,0:T(8,128)(2,1)} fusion(bf16[256,2048]{1,0:T(8,128)(2,1)S(1)} %copy-done, s32[1024]{0:T(1024)S(1)} %eq.29), kind=kOutput, calls=%fused_computation.2 | convolution fusion | flops 1076101120 | bytes 5246976 | tf_op jit(solution)/shard_map/dot_general | solution.py:116
  31.2 6.1 %fusion.4.own_ref = bf16[256,2048]{1,0:T(8,128)(2,1)S(1)} fusion(bf16[256,2048]{1,0:T(8,128)(2,1)S(1)} %bitcast.55, bf16[2048,2048]{1,0:T(8,128)(2,1)} %param.6, bf16[1024,2048]{1,0:T(8,128)(2,1)} %convolution_convert_fusion, f32[256]{0:T(256)S(1)} %bitcast.71), kind=kOutput, calls=%fused_computation.11 | convolution fusion | flops 2150105088 | bytes 11535360 | tf_op jit(solution)/shard_map/dot_general | solution.py:121
  39.5 3.8 %collective-permute-start.9 = (bf16[128,2048]{1,0:T(8,128)(2,1)S(1)}, bf16[128,2048]{1,0:T(8,128)(2,1)S(1)}, u32[]{:S(2)}, u32[]{:S(2)}) collective-permute-start(bf16[128,2048]{1,0:T(8,128)(2,1)S(1)} %slice.94), channel_id=1, source_target_pairs={{0,48},{1,49},{2,50},{3,51},{4,52},{5,53},{6,54},{7,55},{8,56},{9,... | collective-permute-start | bytes 1572872 | tf_op jit(solution)/shard_map/ppermute | solution.py:20
  44.4 2.4 %fusion.5.own_ref = bf16[256,2048]{1,0:T(8,128)(2,1)S(1)} fusion(bf16[256,2048]{1,0:T(8,128)(2,1)S(1)} %collective-permute-done.7.e1, bf16[2048,2048]{1,0:T(8,128)(2,1)S(1)} %bitcast.73, bf16[1024,2048]{1,0:T(8,128)(2,1)S(1)} %copy-done.1, f32[256]{0:T(256)S(1)} %bitcast.70), kind=kOutput, calls=%fused_computation.12 | convolution fusion | flops 2150105088 | bytes 11535360 | tf_op jit(solution)/shard_map/dot_general | solution.py:121
  46.9 3.6 %fusion.7.own_ref = bf16[256,2048]{1,0:T(8,128)(2,1)S(1)} fusion(bf16[256,2048]{1,0:T(8,128)(2,1)} %collective-permute-done.10.e3, bf16[2048,2048]{1,0:T(8,128)(2,1)S(1)} %bitcast.73, bf16[1024,2048]{1,0:T(8,128)(2,1)S(1)} %copy-done.1, f32[256]{0:T(256)S(1)} %bitcast.69), kind=kOutput, calls=%fused_computation.14 | convolution fusion | flops 2150105088 | bytes 11535360 | tf_op jit(solution)/shard_map/dot_general | solution.py:121
  51.3 3.5 %collective-permute-done.11 = bf16[128,2048]{1,0:T(8,128)(2,1)S(1)} collective-permute-done((bf16[128,2048]{1,0:T(8,128)(2,1)S(1)}, bf16[128,2048]{1,0:T(8,128)(2,1)S(1)}, u32[]{:S(2)}, u32[]{:S(2)}) %collective-permute-start.11) | collective-permute-done | bytes 524320 | tf_op jit(solution)/shard_map/ppermute | solution.py:20
  54.8 2.4 %fusion.6.own_ref = bf16[256,2048]{1,0:T(8,128)(2,1)S(1)} fusion(bf16[256,2048]{1,0:T(8,128)(2,1)S(1)} %constant_dynamic-update-slice_fusion.e2, bf16[2048,2048]{1,0:T(8,128)(2,1)S(1)} %bitcast.73, bf16[1024,2048]{1,0:T(8,128)(2,1)S(1)} %copy-done.1, f32[256]{0:T(256)S(1)} %bitcast.68), kind=kOutput, calls=%fused_computation.13 | convolution fusion | flops 2150105088 | bytes 11535360 | tf_op jit(solution)/shard_map/dot_general | solution.py:121
  57.3 2.6 %collective-permute-done.12 = bf16[256,2048]{1,0:T(8,128)(2,1)S(1)} collective-permute-done((bf16[256,2048]{1,0:T(8,128)(2,1)S(1)}, bf16[256,2048]{1,0:T(8,128)(2,1)S(1)}, u32[]{:S(2)}, u32[]{:S(2)}) %collective-permute-start.12) | collective-permute-done | bytes 1048608 | tf_op jit(solution)/shard_map/ppermute | solution.py:28
  61.5 2.4 %convolution_convert_fusion.3 = bf16[256,2048]{1,0:T(8,128)(2,1)S(1)} fusion(bf16[256,2048]{1,0:T(8,128)(2,1)S(1)} %residual.5.r1, bf16[2048,2048]{1,0:T(8,128)(2,1)S(1)} %bitcast.73), kind=kOutput, calls=%fused_computation.17 | convolution fusion | flops 2148007936 | bytes 10485760 | tf_op jit(solution)/shard_map/dot_general | solution.py:129
  63.9 3.3 %convolution_convert_fusion.2 = bf16[256,2048]{1,0:T(8,128)(2,1)} fusion(bf16[256,2048]{1,0:T(8,128)(2,1)S(1)} %residual.6.r2, bf16[2048,2048]{1,0:T(8,128)(2,1)S(1)} %bitcast.73), kind=kOutput, calls=%fused_computation.16 | convolution fusion | flops 2148007936 | bytes 10485760 | tf_op jit(solution)/shard_map/dot_general | solution.py:129
  68.4 3.3 %convolution_convert_fusion.1 = bf16[256,2048]{1,0:T(8,128)(2,1)} fusion(bf16[256,2048]{1,0:T(8,128)(2,1)S(1)} %residual.7.r3, bf16[2048,2048]{1,0:T(8,128)(2,1)S(1)} %bitcast.73), kind=kOutput, calls=%fused_computation.15 | convolution fusion | flops 2148007936 | bytes 10485760 | tf_op jit(solution)/shard_map/dot_general | solution.py:129
  71.8 2.1 %collective-permute-start.16 = (bf16[256,2048]{1,0:T(8,128)(2,1)}, bf16[256,2048]{1,0:T(8,128)(2,1)S(1)}, u32[]{:S(2)}, u32[]{:S(2)}) collective-permute-start(bf16[256,2048]{1,0:T(8,128)(2,1)} %convolution_convert_fusion.1), channel_id=1, source_target_pairs={{0,48},{1,49},{2,50},{3,51},{4,52},{5,53},{6,54},{7,55},{8,56},{9,... | collective-permute-start | bytes 3145736 | tf_op jit(solution)/shard_map/ppermute | solution.py:20
  74.4 2.4 %fusion.26 = f32[256,2048]{1,0:T(8,128)S(1)} fusion(bf16[256,2048]{1,0:T(8,128)(2,1)S(1)} %residual.4.r0, bf16[2048,2048]{1,0:T(8,128)(2,1)S(1)} %bitcast.73), kind=kOutput, calls=%fused_computation.68 | convolution fusion | flops 2147483648 | bytes 11534336 | tf_op jit(solution)/shard_map/dot_general | solution.py:129
  76.7 14.5 %collective-permute-done.14 = bf16[256,2048]{1,0:T(8,128)(2,1)S(1)} collective-permute-done((bf16[256,2048]{1,0:T(8,128)(2,1)S(1)}, bf16[256,2048]{1,0:T(8,128)(2,1)S(1)}, u32[]{:S(2)}, u32[]{:S(2)}) %collective-permute-start.14) | collective-permute-done | bytes 1048608 | tf_op jit(solution)/shard_map/ppermute | solution.py:20
  91.2 4.4 %collective-permute-done.16 = bf16[256,2048]{1,0:T(8,128)(2,1)S(1)} collective-permute-done((bf16[256,2048]{1,0:T(8,128)(2,1)}, bf16[256,2048]{1,0:T(8,128)(2,1)S(1)}, u32[]{:S(2)}, u32[]{:S(2)}) %collective-permute-start.16) | collective-permute-done | bytes 1048608 | tf_op jit(solution)/shard_map/ppermute | solution.py:20
  98.0 2.0 %collective-permute-start.18 = (bf16[64,2048]{1,0:T(8,128)(2,1)S(1)}, bf16[64,2048]{1,0:T(8,128)(2,1)S(1)}, u32[]{:S(2)}, u32[]{:S(2)}) collective-permute-start(bf16[64,2048]{1,0:T(8,128)(2,1)S(1)} %get-tuple-element.12), channel_id=1, source_target_pairs={{0,8},{1,9},{2,10},{3,11},{4,12},{5,13},{6,14},{7,15},{8,0},{9,1},... | collective-permute-start | bytes 786440 | tf_op jit(solution)/shard_map/ppermute | solution.py:20
  100.7 3.3 %collective-permute-done.17 = bf16[64,2048]{1,0:T(8,128)(2,1)S(1)} collective-permute-done((bf16[64,2048]{1,0:T(8,128)(2,1)S(1)}, bf16[64,2048]{1,0:T(8,128)(2,1)S(1)}, u32[]{:S(2)}, u32[]{:S(2)}) %collective-permute-start.17) | collective-permute-done | bytes 262176 | tf_op jit(solution)/shard_map/ppermute | solution.py:20
  104.0 3.1 %collective-permute-done.18 = bf16[64,2048]{1,0:T(8,128)(2,1)S(1)} collective-permute-done((bf16[64,2048]{1,0:T(8,128)(2,1)S(1)}, bf16[64,2048]{1,0:T(8,128)(2,1)S(1)}, u32[]{:S(2)}, u32[]{:S(2)}) %collective-permute-start.18) | collective-permute-done | bytes 262176 | tf_op jit(solution)/shard_map/ppermute | solution.py:20
  108.0 2.0 %collective-permute-start.21 = (bf16[16,2048]{1,0:T(8,128)(2,1)S(1)}, bf16[16,2048]{1,0:T(8,128)(2,1)S(1)}, u32[]{:S(2)}, u32[]{:S(2)}) collective-permute-start(bf16[16,2048]{1,0:T(8,128)(2,1)S(1)} %get-tuple-element.15), channel_id=1, source_target_pairs={{0,2},{1,3},{2,0},{3,1},{4,6},{5,7},{6,4},{7,5},{8,10},{9,11},{10,... | collective-permute-start | bytes 196616 | tf_op jit(solution)/shard_map/ppermute | solution.py:20
  111.9 13.3 %slab_grad.1 = f32[2048,2048]{1,0:T(8,128)} custom-call(bf16[256,2048]{1,0:T(8,128)(2,1)S(1)} %bitcast.56, bf16[256,2048]{1,0:T(8,128)(2,1)S(1)} %collective-permute-done.7.e1, bf16[256,2048]{1,0:T(8,128)(2,1)S(1)} %constant_dynamic-update-slice_fusion.e2, bf16[256,2048]{1,0:T(8,128)(2,1)} %collective-permute-done.10.e3, bf16[256,2048]{1,0:T(8,128)(2,1)S(1)} %residual.4.r0, ...), custom_call_target="tpu_custom_call" | custom-call | flops 8589934592 | bytes 25165824 | tf_op jit(solution)/shard_map/slab_grad/pallas_call | solution.py:85
  (67 shorter events, 27.1 us)
Async XLA Ops:
  0.6 26.5 %copy-start = (bf16[256,2048]{1,0:T(8,128)(2,1)S(1)}, bf16[256,2048]{1,0:T(8,128)(2,1)}, u32[]{:S(2)}) copy-start(bf16[256,2048]{1,0:T(8,128)(2,1)} %param.7) | copy-start | bytes 3145732
  0.6 5.5 %collective-permute-start = (bf16[16,2048]{1,0:T(8,128)(2,1)}, bf16[16,2048]{1,0:T(8,128)(2,1)S(1)}, u32[]{:S(2)}, u32[]{:S(2)}) collective-permute-start(bf16[16,2048]{1,0:T(8,128)(2,1)} %param.5), channel_id=1, source_target_pairs={{0,3},{1,0},{2,1},{3,2},{4,7},{5,4},{6,5},{7,6},{8,11},{9,8},{10,9... | collective-permute-start | bytes 196616 | tf_op jit(solution)/shard_map/ppermute | solution.py:20
  3.6 6.0 %collective-permute-start.1 = (bf16[16,2048]{1,0:T(8,128)(2,1)}, bf16[16,2048]{1,0:T(8,128)(2,1)S(1)}, u32[]{:S(2)}, u32[]{:S(2)}) collective-permute-start(bf16[16,2048]{1,0:T(8,128)(2,1)} %param.5), channel_id=1, source_target_pairs={{0,2},{1,3},{2,0},{3,1},{4,6},{5,7},{6,4},{7,5},{8,10},{9,11},{10,... | collective-permute-start | bytes 196616 | tf_op jit(solution)/shard_map/ppermute | solution.py:20
  4.4 5.9 %collective-permute-start.2 = (bf16[16,2048]{1,0:T(8,128)(2,1)}, bf16[16,2048]{1,0:T(8,128)(2,1)S(1)}, u32[]{:S(2)}, u32[]{:S(2)}) collective-permute-start(bf16[16,2048]{1,0:T(8,128)(2,1)} %param.5), channel_id=1, source_target_pairs={{0,1},{1,2},{2,3},{3,0},{4,5},{5,6},{6,7},{7,4},{8,9},{9,10},{10,1... | collective-permute-start | bytes 196616 | tf_op jit(solution)/shard_map/ppermute | solution.py:20
  11.1 7.7 %collective-permute-start.5 = (bf16[64,2048]{1,0:T(8,128)(2,1)S(1)}, bf16[64,2048]{1,0:T(8,128)(2,1)S(1)}, u32[]{:S(2)}, u32[]{:S(2)}) collective-permute-start(bf16[64,2048]{1,0:T(8,128)(2,1)S(1)} %bitcast.57), channel_id=1, source_target_pairs={{0,4},{1,5},{2,6},{3,7},{4,8},{5,9},{6,10},{7,11},{8,12},{9,13},{1... | collective-permute-start | bytes 786440 | tf_op jit(solution)/shard_map/ppermute | solution.py:20
  12.8 6.4 %collective-permute-start.3 = (bf16[64,2048]{1,0:T(8,128)(2,1)S(1)}, bf16[64,2048]{1,0:T(8,128)(2,1)S(1)}, u32[]{:S(2)}, u32[]{:S(2)}) collective-permute-start(bf16[64,2048]{1,0:T(8,128)(2,1)S(1)} %bitcast.58), channel_id=1, source_target_pairs={{0,12},{1,13},{2,14},{3,15},{4,0},{5,1},{6,2},{7,3},{8,4},{9,5},{1... | collective-permute-start | bytes 786440 | tf_op jit(solution)/shard_map/ppermute | solution.py:20
  14.4 8.4 %collective-permute-start.4 = (bf16[64,2048]{1,0:T(8,128)(2,1)S(1)}, bf16[64,2048]{1,0:T(8,128)(2,1)S(1)}, u32[]{:S(2)}, u32[]{:S(2)}) collective-permute-start(bf16[64,2048]{1,0:T(8,128)(2,1)S(1)} %bitcast.59), channel_id=1, source_target_pairs={{0,8},{1,9},{2,10},{3,11},{4,12},{5,13},{6,14},{7,15},{8,0},{9,1},... | collective-permute-start | bytes 786440 | tf_op jit(solution)/shard_map/ppermute | solution.py:20
  23.0 16.4 %collective-permute-start.7 = (bf16[256,2048]{1,0:T(8,128)(2,1)S(1)}, bf16[256,2048]{1,0:T(8,128)(2,1)S(1)}, u32[]{:S(2)}, u32[]{:S(2)}) collective-permute-start(bf16[256,2048]{1,0:T(8,128)(2,1)S(1)} %bitcast.53), channel_id=1, source_target_pairs={{0,48},{1,49},{2,50},{3,51},{4,52},{5,53},{6,54},{7,55},{8,56},{9,... | collective-permute-start | bytes 3145736 | tf_op jit(solution)/shard_map/ppermute | solution.py:20
  27.1 16.1 %collective-permute-start.10 = (bf16[256,2048]{1,0:T(8,128)(2,1)S(1)}, bf16[256,2048]{1,0:T(8,128)(2,1)}, u32[]{:S(2)}, u32[]{:S(2)}) collective-permute-start(bf16[256,2048]{1,0:T(8,128)(2,1)S(1)} %bitcast.54), channel_id=1, source_target_pairs={{0,16},{1,17},{2,18},{3,19},{4,20},{5,21},{6,22},{7,23},{8,24},{9,... | collective-permute-start | bytes 3145736 | tf_op jit(solution)/shard_map/ppermute | solution.py:20
  37.3 19.9 %collective-permute-start.6 = (bf16[256,2048]{1,0:T(8,128)(2,1)S(1)}, bf16[256,2048]{1,0:T(8,128)(2,1)S(1)}, u32[]{:S(2)}, u32[]{:S(2)}) collective-permute-start(bf16[256,2048]{1,0:T(8,128)(2,1)S(1)} %fusion.4.own_ref), channel_id=1, source_target_pairs={{0,64},{64,0},{1,65},{65,1},{2,66},{66,2},{3,67},{67,3},{4,68},{68... | collective-permute-start | bytes 3145736 | tf_op jit(solution)/shard_map/ppermute | solution.py:28
  39.5 11.8 %collective-permute-start.9 = (bf16[128,2048]{1,0:T(8,128)(2,1)S(1)}, bf16[128,2048]{1,0:T(8,128)(2,1)S(1)}, u32[]{:S(2)}, u32[]{:S(2)}) collective-permute-start(bf16[128,2048]{1,0:T(8,128)(2,1)S(1)} %slice.94), channel_id=1, source_target_pairs={{0,48},{1,49},{2,50},{3,51},{4,52},{5,53},{6,54},{7,55},{8,56},{9,... | collective-permute-start | bytes 1572872 | tf_op jit(solution)/shard_map/ppermute | solution.py:20
  44.3 10.5 %collective-permute-start.11 = (bf16[128,2048]{1,0:T(8,128)(2,1)S(1)}, bf16[128,2048]{1,0:T(8,128)(2,1)S(1)}, u32[]{:S(2)}, u32[]{:S(2)}) collective-permute-start(bf16[128,2048]{1,0:T(8,128)(2,1)S(1)} %slice.95), channel_id=1, source_target_pairs={{0,16},{1,17},{2,18},{3,19},{4,20},{5,21},{6,22},{7,23},{8,24},{9,... | collective-permute-start | bytes 1572872 | tf_op jit(solution)/shard_map/ppermute | solution.py:20
  46.8 10.5 %collective-permute-start.8 = (bf16[256,2048]{1,0:T(8,128)(2,1)S(1)}, bf16[256,2048]{1,0:T(8,128)(2,1)S(1)}, u32[]{:S(2)}, u32[]{:S(2)}) collective-permute-start(bf16[256,2048]{1,0:T(8,128)(2,1)S(1)} %fusion.5.own_ref), channel_id=1, source_target_pairs={{0,64},{64,0},{1,65},{65,1},{2,66},{66,2},{3,67},{67,3},{4,68},{68... | collective-permute-start | bytes 3145736 | tf_op jit(solution)/shard_map/ppermute | solution.py:28
  50.5 6.8 %collective-permute-start.13 = (bf16[256,2048]{1,0:T(8,128)(2,1)S(1)}, bf16[256,2048]{1,0:T(8,128)(2,1)S(1)}, u32[]{:S(2)}, u32[]{:S(2)}) collective-permute-start(bf16[256,2048]{1,0:T(8,128)(2,1)S(1)} %fusion.7.own_ref), channel_id=1, source_target_pairs={{0,64},{64,0},{1,65},{65,1},{2,66},{66,2},{3,67},{67,3},{4,68},{68... | collective-permute-start | bytes 3145736 | tf_op jit(solution)/shard_map/ppermute | solution.py:28
  57.2 2.7 %collective-permute-start.12 = (bf16[256,2048]{1,0:T(8,128)(2,1)S(1)}, bf16[256,2048]{1,0:T(8,128)(2,1)S(1)}, u32[]{:S(2)}, u32[]{:S(2)}) collective-permute-start(bf16[256,2048]{1,0:T(8,128)(2,1)S(1)} %fusion.6.own_ref), channel_id=1, source_target_pairs={{0,64},{64,0},{1,65},{65,1},{2,66},{66,2},{3,67},{67,3},{4,68},{68... | collective-permute-start | bytes 3145736 | tf_op jit(solution)/shard_map/ppermute | solution.py:28
  63.9 27.3 %collective-permute-start.14 = (bf16[256,2048]{1,0:T(8,128)(2,1)S(1)}, bf16[256,2048]{1,0:T(8,128)(2,1)S(1)}, u32[]{:S(2)}, u32[]{:S(2)}) collective-permute-start(bf16[256,2048]{1,0:T(8,128)(2,1)S(1)} %convolution_convert_fusion.3), channel_id=1, source_target_pairs={{0,16},{1,17},{2,18},{3,19},{4,20},{5,21},{6,22},{7,23},{8,24},{9,... | collective-permute-start | bytes 3145736 | tf_op jit(solution)/shard_map/ppermute | solution.py:20
  67.3 23.9 %collective-permute-start.15 = (bf16[256,2048]{1,0:T(8,128)(2,1)}, bf16[256,2048]{1,0:T(8,128)(2,1)S(1)}, u32[]{:S(2)}, u32[]{:S(2)}) collective-permute-start(bf16[256,2048]{1,0:T(8,128)(2,1)} %convolution_convert_fusion.2), channel_id=1, source_target_pairs={{0,32},{1,33},{2,34},{3,35},{4,36},{5,37},{6,38},{7,39},{8,40},{9,... | collective-permute-start | bytes 3145736 | tf_op jit(solution)/shard_map/ppermute | solution.py:20
  71.8 23.8 %collective-permute-start.16 = (bf16[256,2048]{1,0:T(8,128)(2,1)}, bf16[256,2048]{1,0:T(8,128)(2,1)S(1)}, u32[]{:S(2)}, u32[]{:S(2)}) collective-permute-start(bf16[256,2048]{1,0:T(8,128)(2,1)} %convolution_convert_fusion.1), channel_id=1, source_target_pairs={{0,48},{1,49},{2,50},{3,51},{4,52},{5,53},{6,54},{7,55},{8,56},{9,... | collective-permute-start | bytes 3145736 | tf_op jit(solution)/shard_map/ppermute | solution.py:20
  96.4 7.7 %collective-permute-start.17 = (bf16[64,2048]{1,0:T(8,128)(2,1)S(1)}, bf16[64,2048]{1,0:T(8,128)(2,1)S(1)}, u32[]{:S(2)}, u32[]{:S(2)}) collective-permute-start(bf16[64,2048]{1,0:T(8,128)(2,1)S(1)} %get-tuple-element.10), channel_id=1, source_target_pairs={{0,4},{1,5},{2,6},{3,7},{4,8},{5,9},{6,10},{7,11},{8,12},{9,13},{1... | collective-permute-start | bytes 786440 | tf_op jit(solution)/shard_map/ppermute | solution.py:20
  98.0 9.2 %collective-permute-start.18 = (bf16[64,2048]{1,0:T(8,128)(2,1)S(1)}, bf16[64,2048]{1,0:T(8,128)(2,1)S(1)}, u32[]{:S(2)}, u32[]{:S(2)}) collective-permute-start(bf16[64,2048]{1,0:T(8,128)(2,1)S(1)} %get-tuple-element.12), channel_id=1, source_target_pairs={{0,8},{1,9},{2,10},{3,11},{4,12},{5,13},{6,14},{7,15},{8,0},{9,1},... | collective-permute-start | bytes 786440 | tf_op jit(solution)/shard_map/ppermute | solution.py:20
  100.0 7.7 %collective-permute-start.19 = (bf16[64,2048]{1,0:T(8,128)(2,1)S(1)}, bf16[64,2048]{1,0:T(8,128)(2,1)S(1)}, u32[]{:S(2)}, u32[]{:S(2)}) collective-permute-start(bf16[64,2048]{1,0:T(8,128)(2,1)S(1)} %get-tuple-element.11), channel_id=1, source_target_pairs={{0,12},{1,13},{2,14},{3,15},{4,0},{5,1},{6,2},{7,3},{8,4},{9,5},{1... | collective-permute-start | bytes 786440 | tf_op jit(solution)/shard_map/ppermute | solution.py:20
  107.9 17.3 %collective-permute-start.20 = (bf16[16,2048]{1,0:T(8,128)(2,1)S(1)}, bf16[16,2048]{1,0:T(8,128)(2,1)S(1)}, u32[]{:S(2)}, u32[]{:S(2)}) collective-permute-start(bf16[16,2048]{1,0:T(8,128)(2,1)S(1)} %get-tuple-element.13), channel_id=1, source_target_pairs={{0,1},{1,2},{2,3},{3,0},{4,5},{5,6},{6,7},{7,4},{8,9},{9,10},{10,1... | collective-permute-start | bytes 196616 | tf_op jit(solution)/shard_map/ppermute | solution.py:20
  108.0 17.3 %collective-permute-start.21 = (bf16[16,2048]{1,0:T(8,128)(2,1)S(1)}, bf16[16,2048]{1,0:T(8,128)(2,1)S(1)}, u32[]{:S(2)}, u32[]{:S(2)}) collective-permute-start(bf16[16,2048]{1,0:T(8,128)(2,1)S(1)} %get-tuple-element.15), channel_id=1, source_target_pairs={{0,2},{1,3},{2,0},{3,1},{4,6},{5,7},{6,4},{7,5},{8,10},{9,11},{10,... | collective-permute-start | bytes 196616 | tf_op jit(solution)/shard_map/ppermute | solution.py:20
  110.0 15.3 %collective-permute-start.22 = (bf16[16,2048]{1,0:T(8,128)(2,1)S(1)}, bf16[16,2048]{1,0:T(8,128)(2,1)S(1)}, u32[]{:S(2)}, u32[]{:S(2)}) collective-permute-start(bf16[16,2048]{1,0:T(8,128)(2,1)S(1)} %get-tuple-element.14), channel_id=1, source_target_pairs={{0,3},{1,0},{2,1},{3,2},{4,7},{5,4},{6,5},{7,6},{8,11},{9,8},{10,9... | collective-permute-start | bytes 196616 | tf_op jit(solution)/shard_map/ppermute | solution.py:20
  (4 other events, 47.1 us)

commit v2 on v0

v2 whole, which is shorter than its diff:
```python
import jax
import jax.numpy as jnp
from jax import lax
from jax.experimental import pallas as pl
from jax.experimental.pallas import tpu as pltpu
from jax.sharding import PartitionSpec as P

STRIDE = {"x": 1, "y": 4, "z": 16}
ORDER = (("x", "y", "z"), ("x", "z", "y"))
SLAB_CUTS = (4, 4)


def hop(value, phase, offset):
    pairs = []
    for core in range(2):
        stride = STRIDE[ORDER[core][phase]]
        for chip in range(64):
            at = (chip // stride) % 4
            to = chip + ((at + offset) % 4 - at) * stride
            pairs.append((core * 64 + chip, core * 64 + to))
    return lax.ppermute(value, ("row", "col"), pairs)


def fetch(value, phase, offset):
    return hop(value, phase, -offset)


def across(value):
    return lax.ppermute(value, "row", [(0, 1), (1, 0)])


def joined(*pieces):
    return jnp.stack(pieces).reshape(-1, pieces[0].shape[1])


def row_order():
    chip = lax.axis_index("col")
    core = lax.axis_index("row")
    ks = lax.broadcasted_iota(jnp.int32, (64,), 0)
    k3, k2, k1 = ks // 16, (ks // 4) % 4, ks % 4
    dz = jnp.where(core == 0, k3, k2)
    dy = jnp.where(core == 0, k2, k3)
    z, y, x = chip // 16, (chip // 4) % 4, chip % 4
    return ((z + dz) % 4) * 16 + ((y + dy) % 4) * 4 + (x + k1) % 4


def place(k3, k2):
    if k3 == 0:
        return 0, k2
    if k3 == 2:
        return (3, k2) if k2 < 2 else (4, k2 - 2)
    return (1 if k2 < 2 else 2), (0 if k3 == 1 else 2) + k2 % 2


EARLY = [(2, 0), (2, 1), (3, 0), (3, 1), *((1, k) for k in range(4)), *((0, k) for k in range(4))]
LATE = [(2, 2), (2, 3), (3, 2), (3, 3)]


def residual_kernel(blocks, used, *refs):
    *refs, out_ref = refs
    own = dict(zip(used, refs[: len(used)]))
    theirs = dict(zip(used, refs[len(used) :]))
    for row, (k3, k2) in enumerate(blocks):
        group, at = place(k3, k2)
        mine = own[group][at * 64 : (at + 1) * 64, :].astype(jnp.float32)
        group, at = place(k2, k3)
        both = mine + theirs[group][at * 64 : (at + 1) * 64, :].astype(jnp.float32)
        out_ref[row * 64 : (row + 1) * 64, :] = both.astype(jnp.bfloat16)


def residual_of(blocks, used, own, theirs):
    width = own[0].shape[1]
    cols = width // 4
    groups = [own[g] for g in used] + [theirs[g] for g in used]
    return pl.pallas_call(
        lambda *refs: residual_kernel(blocks, used, *refs),
        grid=(width // cols,),
        in_specs=[pl.BlockSpec((g.shape[0], cols), lambda j: (0, j)) for g in groups],
        out_specs=pl.BlockSpec((64 * len(blocks), cols), lambda j: (0, j)),
        out_shape=jax.ShapeDtypeStruct((64 * len(blocks), width), jnp.bfloat16),
        compiler_params=pltpu.CompilerParams(vmem_limit_bytes=10 * 2**20),
        cost_estimate=pl.CostEstimate(
            flops=64 * 64 * len(blocks) * width, bytes_accessed=6 * 64 * len(blocks) * width, transcendentals=0
        ),
        name="residual",
    )(*groups)


def slab_kernel(count, *refs):
    e_refs, early_ref, late_ref = refs[:count], refs[count], refs[count + 1]
    out_ref, e_early, e_late = refs[-3:]
    row = 0
    rows = early_ref.shape[0]
    for ref in e_refs:
        size = ref.shape[0]
        if row < rows:
            e_early[row : row + size, :] = ref[...]
        else:
            e_late[row - rows : row - rows + size, :] = ref[...]
        row += size
    dims = (((0,), (0,)), ((), ()))
    out_ref[...] = lax.dot_general(
        e_early[...], early_ref[...], dims, preferred_element_type=jnp.float32
    ) + lax.dot_general(e_late[...], late_ref[...], dims, preferred_element_type=jnp.float32)


def slab_product(pieces, early, late, whole, first, count):
    hidden = pieces[0].shape[1]
    width = early.shape[1]
    rows = early.shape[0] + late.shape[0]
    block = hidden // 8
    given = () if whole is None else (whole,)
    return pl.pallas_call(
        lambda *refs: slab_kernel(len(pieces), *refs),
        grid=(count,),
        in_specs=[pl.BlockSpec((p.shape[0], block), lambda i: (0, first + i)) for p in pieces]
        + [pl.BlockSpec(r.shape, lambda i: (0, 0), pipeline_mode=pl.Buffered(1)) for r in (early, late)]
        + [pl.BlockSpec(memory_space=pl.ANY)] * len(given),
        out_specs=pl.BlockSpec((block, width), lambda i: (first + i, 0)),
        out_shape=jax.ShapeDtypeStruct((hidden, width), jnp.float32),
        scratch_shapes=[
            pltpu.VMEM((early.shape[0], block), jnp.bfloat16),
            pltpu.VMEM((late.shape[0], block), jnp.bfloat16),
        ],
        input_output_aliases={len(pieces) + 2: 0} if given else {},
        compiler_params=pltpu.CompilerParams(dimension_semantics=("arbitrary",), vmem_limit_bytes=20 * 2**20),
        cost_estimate=pl.CostEstimate(
            flops=2 * rows * block * count * width, bytes_accessed=count * 5 * 2**19 + 2**22, transcendentals=0
        ),
        name="slab_grad",
    )(*pieces, early, late, *given)


def stage_kernel(source_ref, out_ref, sem):
    copy = pltpu.make_async_copy(source_ref, out_ref, sem)
    copy.start()
    copy.wait()


def staged(value):
    return pl.pallas_call(
        stage_kernel,
        in_specs=[pl.BlockSpec(memory_space=pltpu.HBM)],
        out_specs=pl.BlockSpec(memory_space=pltpu.VMEM),
        out_shape=pltpu.VMEM(value.shape, value.dtype),
        scratch_shapes=[pltpu.SemaphoreType.DMA],
        compiler_params=pltpu.CompilerParams(vmem_limit_bytes=2**20),
        cost_estimate=pl.CostEstimate(flops=64 * value.size, bytes_accessed=2 * value.size, transcendentals=0),
        name="bring_in",
    )(value)


def times_transpose(name, rows, slab_weight):
    part = lax.dot_general(
        rows, slab_weight, (((1,), (1,)), ((), ())), preferred_element_type=jnp.float32
    )
    return lax.optimization_barrier(part if name == "back0" else part.astype(jnp.bfloat16))


def plus(mine, came):
    return (mine.astype(jnp.float32) + came.astype(jnp.float32)).astype(jnp.bfloat16)


def body(embeddings, slab_weight, target_table, client_ids, client_weights):
    block = row_order()
    ids = client_ids.reshape(64, 16)[block].reshape(-1)
    weights = client_weights.reshape(64, 16)[block].reshape(-1)
    picks = (ids[:, None] == lax.broadcasted_iota(jnp.int32, (1, target_table.shape[0]), 1)).astype(jnp.bfloat16)
    picks, weights = lax.optimization_barrier((picks, weights))
    slab_weight = staged(slab_weight)

    nearby = staged(embeddings)
    value = joined(nearby, *(fetch(embeddings, 0, k) for k in (1, 2, 3)))
    ring = [value, *(fetch(value, 1, k) for k in (1, 2, 3))]
    top, low = joined(*ring[:2]), joined(*ring[2:])
    half = top.shape[0]
    top1 = fetch(top, 2, 1)
    top3 = fetch(top, 2, 3)
    low3 = fetch(low, 2, 3)
    low1 = fetch(low, 2, 1)
    top2 = fetch(top1, 2, 1)
    low2 = fetch(low3, 2, 3)
    target = jnp.dot(picks, target_table, preferred_element_type=jnp.float32).astype(jnp.bfloat16)
    target = lax.optimization_barrier(target)

    groups = [joined(*ring), joined(top1, top3), joined(low1, low3), top2, low2]
    own, theirs = [], []
    for g, rows in enumerate(groups):
        spans = {0: (0,), 1: (2, 6), 2: (3, 7), 3: (4,), 4: (5,)}[g]
        size = rows.shape[0] // len(spans)
        scale = jnp.concatenate([weights[s * half : s * half + size] for s in spans])[:, None]
        wanted = jnp.concatenate([target[s * half : s * half + size] for s in spans])
        part = jnp.dot(rows, slab_weight, preferred_element_type=jnp.float32)
        own.append((scale * (part - 0.5 * wanted.astype(jnp.float32))).astype(jnp.bfloat16))
        theirs.append(across(own[g]))

    early = residual_of(EARLY, (0, 1, 2, 3), own, theirs)
    back_a = times_transpose("back_a", early[: 2 * half], slab_weight)
    far_top = hop(back_a[:half], 2, 3)
    back1 = times_transpose("back1", early[2 * half : 4 * half], slab_weight)
    back0 = times_transpose("back0", early[4 * half :], slab_weight)
    late = residual_of(LATE, (2, 4), own, theirs)
    back_b = times_transpose("back_b", late, slab_weight)
    far_low = hop(back_b[:half], 2, 1)
    low_from3 = hop(back_b[half:], 2, 3)
    top_from1 = hop(back1[:half], 2, 1)
    top_from3 = hop(plus(back_a[half:], far_top), 2, 3)
    low_from1 = hop(plus(back1[half:], far_low), 2, 1)

    pieces = [top2, top3, top1, low1, groups[0], low2, low3]
    slab_grad, first = None, 0
    for count in SLAB_CUTS:
        slab_grad = slab_product(pieces, early, late, slab_grad, first, count)
        first += count

    total = jnp.concatenate(
        [
            back0[:half] + top_from1.astype(jnp.float32) + top_from3.astype(jnp.float32),
            back0[half:] + low_from1.astype(jnp.float32) + low_from3.astype(jnp.float32),
        ]
    )
    for phase in (1, 0):
        cut = total.reshape(4, -1, total.shape[-1])
        total = cut[0]
        for k in (1, 2, 3):
            total = total + hop(cut[k].astype(jnp.bfloat16), phase, k).astype(jnp.float32)
    return total, slab_grad


def solution(mesh):
    placed = (P("col", "row"), P("row", "col"), P(None, "col"), P(), P())
    return jax.shard_map(
        body,
        mesh=mesh,
        in_specs=placed,
        out_specs=(P("col", "row"), P("row", "col")),
        check_vma=False,
    )
```

time: 221 us -> 117 us (0.53)
  waiting for transfers between devices: 110 us -> 31.6 us
  starting transfers between devices: 10.7 us -> 40.4 us
  matrix products: 43.3 us -> 20.4 us
  local copies, waits for them, and re-layouts: 24.4 us -> 4.51 us
  Pallas kernels: 0 us -> 16.4 us
  other arithmetic: 17.9 us -> 2.22 us
  between operations: 14.1 us -> 1.06 us
    all_gather x2 -> x0, waiting for transfers between devices: 87.4 us -> none  [the longest x1 74 us: per_device(): features = lax.all_gather(embeddings, 'col', axis=0, tiled=True)]
    ppermute x0 -> x29, starting transfers between devices: none -> 40.4 us  [the longest x24 39.9 us: hop(): return lax.ppermute(value, ('row', 'col'), pairs)]
    ppermute x0 -> x29, waiting for transfers between devices: none -> 31.6 us  [the longest x24 31.6 us: hop(): return lax.ppermute(value, ('row', 'col'), pairs)]
    dot_general x3 -> x10, matrix products: 43.3 us -> 20.4 us  [the longest x5 9.68 us: body(): part = jnp.dot(rows, slab_weight, preferred_element_type=jnp.float32)]
    all_to_all x1 -> x0, waiting for transfers between devices: 21.7 us -> none  [summed_on_arrival(): pieces = lax.all_to_all(cut_along(value, dim, size), axis, 0, 0, tiled=True)]
    unnamed x13 -> x10, local copies, waits for them, and re-layouts: 18.4 us -> 1.16 us
    pallas_call x0 -> x6, Pallas kernels: none -> 16.4 us  [the longest x2 13.6 us: slab_product(): pl.pallas_call(lambda *refs: slab_kernel(len(pieces), *refs), grid=(count...]
    reduce_sum x2 -> x0, other arithmetic: 13.5 us -> none  [the longest x1 10 us: total_of_pieces(): return pieces.sum(axis=0)]
  transfers between devices with their start and end apart: 3 -> 29, of which waited for: 3 -> 11; matrix products, arithmetic and copies ran while one was open for 18% -> 21% of each run, Pallas kernels for 0% -> 14%
where the time goes in v2:
time: 117 us
  starting transfers between devices  40.4 us (35%)
  waiting for transfers between devices  31.6 us (27%)
  matrix products  20.4 us (17%)
  Pallas kernels  16.4 us (14%)
  local copies, waits for them, and re-layouts  4.51 us (4%)
  other arithmetic  2.22 us (2%)
    ppermute x24, starting transfers between devices, hop(): return lax.ppermute(value, ('row', 'col'), pairs)  39.9 us
    ppermute x24, waiting for transfers between devices, hop(): return lax.ppermute(value, ('row', 'col'), pairs)  31.6 us
    pallas_call x2, Pallas kernels, slab_product(): pl.pallas_call(lambda *refs: slab_kernel(len(pieces), *refs), grid=(count...  13.6 us
    dot_general x5, matrix products, body(): part = jnp.dot(rows, slab_weight, preferred_element_type=jnp.float32)  9.68 us
    dot_general x4, matrix products, times_transpose(): lax.dot_general(rows, slab_weight, (((1,), (1,)), ((), ())), preferred_el...  9.45 us
  transfers between devices with their start and end apart: 29, of which 11 were waited for; matrix products, arithmetic and copies ran while one was open for 21% of the time, Pallas kernels for 14%

profile of v2, /device:TPU:0, one launch (start us, length us, event | category | flops | bytes accessed | tf_op | source)
XLA Modules:
  0.0 116.6 jit_solution(2259364407462614056)
XLA Ops:
  0.6 2.9 %collective-permute-start = (bf16[16,2048]{1,0:T(8,128)(2,1)}, bf16[16,2048]{1,0:T(8,128)(2,1)S(1)}, u32[]{:S(2)}, u32[]{:S(2)}) collective-permute-start(bf16[16,2048]{1,0:T(8,128)(2,1)} %source_ref.2), channel_id=1, source_target_pairs={{0,3},{1,0},{2,1},{3,2},{4,7},{5,4},{6,5},{7,6},{8,11},{9,8},{10,9... | collective-permute-start | bytes 196616 | tf_op jit(solution)/shard_map/ppermute | solution.py:21
  3.6 2.3 %collective-permute-start.1 = (bf16[16,2048]{1,0:T(8,128)(2,1)}, bf16[16,2048]{1,0:T(8,128)(2,1)S(1)}, u32[]{:S(2)}, u32[]{:S(2)}) collective-permute-start(bf16[16,2048]{1,0:T(8,128)(2,1)} %source_ref.2), channel_id=1, source_target_pairs={{0,2},{1,3},{2,0},{3,1},{4,6},{5,7},{6,4},{7,5},{8,10},{9,11},{10,... | collective-permute-start | bytes 196616 | tf_op jit(solution)/shard_map/ppermute | solution.py:21
  11.8 3.1 %collective-permute-start.3 = (bf16[64,2048]{1,0:T(8,128)(2,1)S(1)}, bf16[64,2048]{1,0:T(8,128)(2,1)S(1)}, u32[]{:S(2)}, u32[]{:S(2)}) collective-permute-start(bf16[64,2048]{1,0:T(8,128)(2,1)S(1)} %bitcast.45), channel_id=1, source_target_pairs={{0,12},{1,13},{2,14},{3,15},{4,0},{5,1},{6,2},{7,3},{8,4},{9,5},{1... | collective-permute-start | bytes 786440 | tf_op jit(solution)/shard_map/ppermute | solution.py:21
  15.0 2.2 %collective-permute-start.4 = (bf16[64,2048]{1,0:T(8,128)(2,1)S(1)}, bf16[64,2048]{1,0:T(8,128)(2,1)S(1)}, u32[]{:S(2)}, u32[]{:S(2)}) collective-permute-start(bf16[64,2048]{1,0:T(8,128)(2,1)S(1)} %bitcast.47), channel_id=1, source_target_pairs={{0,8},{1,9},{2,10},{3,11},{4,12},{5,13},{6,14},{7,15},{8,0},{9,1},... | collective-permute-start | bytes 786440 | tf_op jit(solution)/shard_map/ppermute | solution.py:21
  18.8 6.5 %collective-permute-done.5 = bf16[64,2048]{1,0:T(8,128)(2,1)S(1)} collective-permute-done((bf16[64,2048]{1,0:T(8,128)(2,1)S(1)}, bf16[64,2048]{1,0:T(8,128)(2,1)S(1)}, u32[]{:S(2)}, u32[]{:S(2)}) %collective-permute-start.5) | collective-permute-done | bytes 262176 | tf_op jit(solution)/shard_map/ppermute | solution.py:21
  25.6 2.7 %collective-permute-start.9 = (bf16[128,2048]{1,0:T(8,128)(2,1)S(1)}, bf16[128,2048]{1,0:T(8,128)(2,1)S(1)}, u32[]{:S(2)}, u32[]{:S(2)}) collective-permute-start(bf16[128,2048]{1,0:T(8,128)(2,1)S(1)} %bitcast.58), channel_id=1, source_target_pairs={{0,16},{1,17},{2,18},{3,19},{4,20},{5,21},{6,22},{7,23},{8,24},{9,... | collective-permute-start | bytes 1572872 | tf_op jit(solution)/shard_map/ppermute | solution.py:21
  30.3 3.2 %collective-permute-start.6 = (bf16[128,2048]{1,0:T(8,128)(2,1)S(1)}, bf16[128,2048]{1,0:T(8,128)(2,1)S(1)}, u32[]{:S(2)}, u32[]{:S(2)}) collective-permute-start(bf16[128,2048]{1,0:T(8,128)(2,1)S(1)} %bitcast.61), channel_id=1, source_target_pairs={{0,48},{1,49},{2,50},{3,51},{4,52},{5,53},{6,54},{7,55},{8,56},{9,... | collective-permute-start | bytes 1572872 | tf_op jit(solution)/shard_map/ppermute | solution.py:21
  33.6 2.4 %fusion.3.refs_0_ = bf16[256,2048]{1,0:T(8,128)(2,1)S(1)} fusion(bf16[256,2048]{1,0:T(8,128)(2,1)S(1)} %bitcast.37, bf16[2048,2048]{1,0:T(8,128)(2,1)S(1)} %bring_in.3, bf16[1024,2048]{1,0:T(8,128)(2,1)S(1)} %convolution_convert_fusion, f32[256]{0:T(256)S(1)} %slice-done), kind=kOutput, calls=%fused_computation.9 | convolution fusion | flops 2150105088 | bytes 11535360 | tf_op jit(solution)/shard_map/dot_general | solution.py:193
  36.0 7.0 %collective-permute-done.7.refs_1_ = bf16[128,2048]{1,0:T(8,128)(2,1)S(1)} collective-permute-done((bf16[128,2048]{1,0:T(8,128)(2,1)S(1)}, bf16[128,2048]{1,0:T(8,128)(2,1)S(1)}, u32[]{:S(2)}, u32[]{:S(2)}) %collective-permute-start.7) | collective-permute-done | bytes 524320 | tf_op jit(solution)/shard_map/ppermute | solution.py:21
  43.1 2.4 %fusion.4.refs_1_ = bf16[256,2048]{1,0:T(8,128)(2,1)S(1)} fusion(bf16[256,2048]{1,0:T(8,128)(2,1)S(1)} %bitcast.51, bf16[2048,2048]{1,0:T(8,128)(2,1)S(1)} %bring_in.3, bf16[128,2048]{1,0:T(8,128)(2,1)S(1)} %get-tuple-element.10, bf16[128,2048]{1,0:T(8,128)(2,1)S(1)} %get-tuple-element.11, f32[256]{0:T(256)S(1)} %pad_maximum_fusion.6), kind=kOutput, calls=%fused_computation.10 | convolution fusion | flops 2151677952 | bytes 11535360 | tf_op jit(solution)/shard_map/dot_general | solution.py:193
  47.5 2.4 %fusion.5.refs_2_.refs_0_ = bf16[256,2048]{1,0:T(8,128)(2,1)S(1)} fusion(bf16[256,2048]{1,0:T(8,128)(2,1)S(1)} %bitcast.50, bf16[2048,2048]{1,0:T(8,128)(2,1)S(1)} %bring_in.3, bf16[128,2048]{1,0:T(8,128)(2,1)S(1)} %get-tuple-element.9, bf16[128,2048]{1,0:T(8,128)(2,1)S(1)} %get-tuple-element.8, f32[256]{0:T(256)S(1)} %pad_maximum_fusion.7), kind=kOutput, calls=%fused_computation.11 | convolution fusion | flops 2151677952 | bytes 11535360 | tf_op jit(solution)/shard_map/dot_general | solution.py:193
  49.9 2.3 %collective-permute-start.10 = (bf16[128,2048]{1,0:T(8,128)(2,1)S(1)}, bf16[128,2048]{1,0:T(8,128)(2,1)S(1)}, u32[]{:S(2)}, u32[]{:S(2)}) collective-permute-start(bf16[128,2048]{1,0:T(8,128)(2,1)S(1)} %collective-permute-done.6.refs_2_), channel_id=1, source_target_pairs={{0,48},{1,49},{2,50},{3,51},{4,52},{5,53},{6,54},{7,55},{8,56},{9,... | collective-permute-start | bytes 1572872 | tf_op jit(solution)/shard_map/ppermute | solution.py:21
  52.2 4.2 %collective-permute-done.19.refs_5_ = bf16[128,2048]{1,0:T(8,128)(2,1)S(1)} collective-permute-done((bf16[128,2048]{1,0:T(8,128)(2,1)S(1)}, bf16[128,2048]{1,0:T(8,128)(2,1)S(1)}, u32[]{:S(2)}, u32[]{:S(2)}) %collective-permute-start.19) | collective-permute-done | bytes 524320 | tf_op jit(solution)/shard_map/ppermute | solution.py:21
  61.3 2.4 %convolution_convert_fusion.1 = bf16[256,2048]{1,0:T(8,128)(2,1)S(1)} fusion(bf16[256,2048]{1,0:T(8,128)(2,1)S(1)} %residual.3.refs_8_, bf16[2048,2048]{1,0:T(8,128)(2,1)S(1)} %bring_in.3), kind=kOutput, calls=%fused_computation.12 | convolution fusion | flops 2148007936 | bytes 10485760 | tf_op jit(solution)/shard_map/dot_general | solution.py:154
  67.3 2.4 %convolution_convert_fusion.2 = bf16[256,2048]{1,0:T(8,128)(2,1)S(1)} fusion(bf16[2048,2048]{1,0:T(8,128)(2,1)S(1)} %bring_in.3, bf16[768,2048]{1,0:T(8,128)(2,1)S(1)} %residual.2.refs_7_), kind=kOutput, calls=%fused_computation.13 | convolution fusion | flops 2148007936 | bytes 10485760 | tf_op jit(solution)/shard_map/dot_general | solution.py:154
  71.6 2.4 %convolution_convert_fusion.3 = bf16[256,2048]{1,0:T(8,128)(2,1)S(1)} fusion(bf16[2048,2048]{1,0:T(8,128)(2,1)S(1)} %bring_in.3, bf16[768,2048]{1,0:T(8,128)(2,1)S(1)} %residual.2.refs_7_), kind=kOutput, calls=%fused_computation.14 | convolution fusion | flops 2148007936 | bytes 10485760 | tf_op jit(solution)/shard_map/dot_general | solution.py:154
  76.1 3.1 %collective-permute-done.16 = bf16[128,2048]{1,0:T(8,128)(2,1)S(1)} collective-permute-done((bf16[128,2048]{1,0:T(8,128)(2,1)S(1)}, bf16[128,2048]{1,0:T(8,128)(2,1)S(1)}, u32[]{:S(2)}, u32[]{:S(2)}) %collective-permute-start.16) | collective-permute-done | bytes 524320 | tf_op jit(solution)/shard_map/ppermute | solution.py:21
  79.4 2.8 %collective-permute-start.17 = (bf16[128,2048]{1,0:T(8,128)(2,1)S(1)}, bf16[128,2048]{1,0:T(8,128)(2,1)S(1)}, u32[]{:S(2)}, u32[]{:S(2)}) collective-permute-start(bf16[128,2048]{1,0:T(8,128)(2,1)S(1)} %add_convert_fusion.1), channel_id=1, source_target_pairs={{0,48},{1,49},{2,50},{3,51},{4,52},{5,53},{6,54},{7,55},{8,56},{9,... | collective-permute-start | bytes 1572872 | tf_op jit(solution)/shard_map/ppermute | solution.py:21
  82.4 2.4 %fusion.15 = f32[256,2048]{1,0:T(8,128)S(1)} fusion(bf16[2048,2048]{1,0:T(8,128)(2,1)S(1)} %bring_in.3, bf16[768,2048]{1,0:T(8,128)(2,1)S(1)} %residual.2.refs_7_), kind=kOutput, calls=%fused_computation.28 | convolution fusion | flops 2147483648 | bytes 11534336 | tf_op jit(solution)/shard_map/dot_general | solution.py:154
  86.5 4.0 %collective-permute-done.17 = bf16[128,2048]{1,0:T(8,128)(2,1)S(1)} collective-permute-done((bf16[128,2048]{1,0:T(8,128)(2,1)S(1)}, bf16[128,2048]{1,0:T(8,128)(2,1)S(1)}, u32[]{:S(2)}, u32[]{:S(2)}) %collective-permute-start.17) | collective-permute-done | bytes 524320 | tf_op jit(solution)/shard_map/ppermute | solution.py:21
  90.5 2.3 %collective-permute-done.22 = bf16[128,2048]{1,0:T(8,128)(2,1)S(1)} collective-permute-done((bf16[128,2048]{1,0:T(8,128)(2,1)S(1)}, bf16[128,2048]{1,0:T(8,128)(2,1)S(1)}, u32[]{:S(2)}, u32[]{:S(2)}) %collective-permute-start.22) | collective-permute-done | bytes 524320 | tf_op jit(solution)/shard_map/ppermute | solution.py:21
  93.4 4.4 %collective-permute-start.24 = (bf16[64,2048]{1,0:T(8,128)(2,1)S(1)}, bf16[64,2048]{1,0:T(8,128)(2,1)S(1)}, u32[]{:S(2)}, u32[]{:S(2)}) collective-permute-start(bf16[64,2048]{1,0:T(8,128)(2,1)S(1)} %get-tuple-element.16), channel_id=1, source_target_pairs={{0,8},{1,9},{2,10},{3,11},{4,12},{5,13},{6,14},{7,15},{8,0},{9,1},... | collective-permute-start | bytes 786440 | tf_op jit(solution)/shard_map/ppermute | solution.py:21
  97.8 6.8 %slab_grad.2.refs_9_ = f32[2048,2048]{1,0:T(8,128)} custom-call(bf16[128,2048]{1,0:T(8,128)(2,1)S(1)} %collective-permute-done.10.refs_0_, bf16[128,2048]{1,0:T(8,128)(2,1)S(1)} %collective-permute-done.7.refs_1_, bf16[128,2048]{1,0:T(8,128)(2,1)S(1)} %collective-permute-done.6.refs_2_, bf16[128,2048]{1,0:T(8,128)(2,1)S(1)} %collective-permute-done.8.refs_3_, ...), custom_call_target="tpu_custom_call" | custom-call | flops 4294967296 | bytes 14680064 | tf_op jit(solution)/shard_map/slab_grad/pallas_call | solution.py:113
  109.1 6.8 %slab_grad.3 = f32[2048,2048]{1,0:T(8,128)} custom-call(bf16[128,2048]{1,0:T(8,128)(2,1)S(1)} %collective-permute-done.10.refs_0_, bf16[128,2048]{1,0:T(8,128)(2,1)S(1)} %collective-permute-done.7.refs_1_, bf16[128,2048]{1,0:T(8,128)(2,1)S(1)} %collective-permute-done.6.refs_2_, ...), custom_call_target="tpu_custom_call", output_to_operand_aliasing={{}: (9, {})} | custom-call | flops 4294967296 | bytes 14680064 | tf_op jit(solution)/shard_map/slab_grad/pallas_call | solution.py:113
  (92 shorter events, 32.5 us)
Async XLA Ops:
  0.6 11.1 %collective-permute-start = (bf16[16,2048]{1,0:T(8,128)(2,1)}, bf16[16,2048]{1,0:T(8,128)(2,1)S(1)}, u32[]{:S(2)}, u32[]{:S(2)}) collective-permute-start(bf16[16,2048]{1,0:T(8,128)(2,1)} %source_ref.2), channel_id=1, source_target_pairs={{0,3},{1,0},{2,1},{3,2},{4,7},{5,4},{6,5},{7,6},{8,11},{9,8},{10,9... | collective-permute-start | bytes 196616 | tf_op jit(solution)/shard_map/ppermute | solution.py:21
  3.6 8.2 %collective-permute-start.2 = (bf16[16,2048]{1,0:T(8,128)(2,1)}, bf16[16,2048]{1,0:T(8,128)(2,1)S(1)}, u32[]{:S(2)}, u32[]{:S(2)}) collective-permute-start(bf16[16,2048]{1,0:T(8,128)(2,1)} %source_ref.2), channel_id=1, source_target_pairs={{0,1},{1,2},{2,3},{3,0},{4,5},{5,6},{6,7},{7,4},{8,9},{9,10},{10,1... | collective-permute-start | bytes 196616 | tf_op jit(solution)/shard_map/ppermute | solution.py:21
  3.6 8.2 %collective-permute-start.1 = (bf16[16,2048]{1,0:T(8,128)(2,1)}, bf16[16,2048]{1,0:T(8,128)(2,1)S(1)}, u32[]{:S(2)}, u32[]{:S(2)}) collective-permute-start(bf16[16,2048]{1,0:T(8,128)(2,1)} %source_ref.2), channel_id=1, source_target_pairs={{0,2},{1,3},{2,0},{3,1},{4,6},{5,7},{6,4},{7,5},{8,10},{9,11},{10,... | collective-permute-start | bytes 196616 | tf_op jit(solution)/shard_map/ppermute | solution.py:21
  14.9 10.5 %collective-permute-start.5 = (bf16[64,2048]{1,0:T(8,128)(2,1)S(1)}, bf16[64,2048]{1,0:T(8,128)(2,1)S(1)}, u32[]{:S(2)}, u32[]{:S(2)}) collective-permute-start(bf16[64,2048]{1,0:T(8,128)(2,1)S(1)} %bitcast.46), channel_id=1, source_target_pairs={{0,4},{1,5},{2,6},{3,7},{4,8},{5,9},{6,10},{7,11},{8,12},{9,13},{1... | collective-permute-start | bytes 786440 | tf_op jit(solution)/shard_map/ppermute | solution.py:21
  15.0 10.4 %collective-permute-start.4 = (bf16[64,2048]{1,0:T(8,128)(2,1)S(1)}, bf16[64,2048]{1,0:T(8,128)(2,1)S(1)}, u32[]{:S(2)}, u32[]{:S(2)}) collective-permute-start(bf16[64,2048]{1,0:T(8,128)(2,1)S(1)} %bitcast.47), channel_id=1, source_target_pairs={{0,8},{1,9},{2,10},{3,11},{4,12},{5,13},{6,14},{7,15},{8,0},{9,1},... | collective-permute-start | bytes 786440 | tf_op jit(solution)/shard_map/ppermute | solution.py:21
  25.6 20.0 %collective-permute-start.9 = (bf16[128,2048]{1,0:T(8,128)(2,1)S(1)}, bf16[128,2048]{1,0:T(8,128)(2,1)S(1)}, u32[]{:S(2)}, u32[]{:S(2)}) collective-permute-start(bf16[128,2048]{1,0:T(8,128)(2,1)S(1)} %bitcast.58), channel_id=1, source_target_pairs={{0,16},{1,17},{2,18},{3,19},{4,20},{5,21},{6,22},{7,23},{8,24},{9,... | collective-permute-start | bytes 1572872 | tf_op jit(solution)/shard_map/ppermute | solution.py:21
  28.2 17.4 %collective-permute-start.8 = (bf16[128,2048]{1,0:T(8,128)(2,1)S(1)}, bf16[128,2048]{1,0:T(8,128)(2,1)S(1)}, u32[]{:S(2)}, u32[]{:S(2)}) collective-permute-start(bf16[128,2048]{1,0:T(8,128)(2,1)S(1)} %bitcast.59), channel_id=1, source_target_pairs={{0,48},{1,49},{2,50},{3,51},{4,52},{5,53},{6,54},{7,55},{8,56},{9,... | collective-permute-start | bytes 1572872 | tf_op jit(solution)/shard_map/ppermute | solution.py:21
  30.3 12.7 %collective-permute-start.7 = (bf16[128,2048]{1,0:T(8,128)(2,1)S(1)}, bf16[128,2048]{1,0:T(8,128)(2,1)S(1)}, u32[]{:S(2)}, u32[]{:S(2)}) collective-permute-start(bf16[128,2048]{1,0:T(8,128)(2,1)S(1)} %bitcast.60), channel_id=1, source_target_pairs={{0,16},{1,17},{2,18},{3,19},{4,20},{5,21},{6,22},{7,23},{8,24},{9,... | collective-permute-start | bytes 1572872 | tf_op jit(solution)/shard_map/ppermute | solution.py:21
  30.3 12.7 %collective-permute-start.6 = (bf16[128,2048]{1,0:T(8,128)(2,1)S(1)}, bf16[128,2048]{1,0:T(8,128)(2,1)S(1)}, u32[]{:S(2)}, u32[]{:S(2)}) collective-permute-start(bf16[128,2048]{1,0:T(8,128)(2,1)S(1)} %bitcast.61), channel_id=1, source_target_pairs={{0,48},{1,49},{2,50},{3,51},{4,52},{5,53},{6,54},{7,55},{8,56},{9,... | collective-permute-start | bytes 1572872 | tf_op jit(solution)/shard_map/ppermute | solution.py:21
  35.9 29.8 %collective-permute-start.11 = (bf16[256,2048]{1,0:T(8,128)(2,1)S(1)}, bf16[256,2048]{1,0:T(8,128)(2,1)S(1)}, u32[]{:S(2)}, u32[]{:S(2)}) collective-permute-start(bf16[256,2048]{1,0:T(8,128)(2,1)S(1)} %fusion.3.refs_0_), channel_id=1, source_target_pairs={{0,64},{64,0},{1,65},{65,1},{2,66},{66,2},{3,67},{67,3},{4,68},{68... | collective-permute-start | bytes 3145736 | tf_op jit(solution)/shard_map/ppermute | solution.py:29
  45.5 20.2 %collective-permute-start.12 = (bf16[256,2048]{1,0:T(8,128)(2,1)S(1)}, bf16[256,2048]{1,0:T(8,128)(2,1)S(1)}, u32[]{:S(2)}, u32[]{:S(2)}) collective-permute-start(bf16[256,2048]{1,0:T(8,128)(2,1)S(1)} %fusion.4.refs_1_), channel_id=1, source_target_pairs={{0,64},{64,0},{1,65},{65,1},{2,66},{66,2},{3,67},{67,3},{4,68},{68... | collective-permute-start | bytes 3145736 | tf_op jit(solution)/shard_map/ppermute | solution.py:29
  45.7 10.7 %collective-permute-start.19 = (bf16[128,2048]{1,0:T(8,128)(2,1)S(1)}, bf16[128,2048]{1,0:T(8,128)(2,1)S(1)}, u32[]{:S(2)}, u32[]{:S(2)}) collective-permute-start(bf16[128,2048]{1,0:T(8,128)(2,1)S(1)} %collective-permute-done.9.refs_6_), channel_id=1, source_target_pairs={{0,16},{1,17},{2,18},{3,19},{4,20},{5,21},{6,22},{7,23},{8,24},{9,... | collective-permute-start | bytes 1572872 | tf_op jit(solution)/shard_map/ppermute | solution.py:21
  49.9 10.8 %collective-permute-start.13 = (bf16[256,2048]{1,0:T(8,128)(2,1)S(1)}, bf16[256,2048]{1,0:T(8,128)(2,1)S(1)}, u32[]{:S(2)}, u32[]{:S(2)}) collective-permute-start(bf16[256,2048]{1,0:T(8,128)(2,1)S(1)} %fusion.5.refs_2_.refs_0_), channel_id=1, source_target_pairs={{0,64},{64,0},{1,65},{65,1},{2,66},{66,2},{3,67},{67,3},{4,68},{68... | collective-permute-start | bytes 3145736 | tf_op jit(solution)/shard_map/ppermute | solution.py:29
  49.9 9.3 %collective-permute-start.10 = (bf16[128,2048]{1,0:T(8,128)(2,1)S(1)}, bf16[128,2048]{1,0:T(8,128)(2,1)S(1)}, u32[]{:S(2)}, u32[]{:S(2)}) collective-permute-start(bf16[128,2048]{1,0:T(8,128)(2,1)S(1)} %collective-permute-done.6.refs_2_), channel_id=1, source_target_pairs={{0,48},{1,49},{2,50},{3,51},{4,52},{5,53},{6,54},{7,55},{8,56},{9,... | collective-permute-start | bytes 1572872 | tf_op jit(solution)/shard_map/ppermute | solution.py:21
  63.7 18.4 %collective-permute-start.21 = (bf16[128,2048]{1,0:T(8,128)(2,1)S(1)}, bf16[128,2048]{1,0:T(8,128)(2,1)S(1)}, u32[]{:S(2)}, u32[]{:S(2)}) collective-permute-start(bf16[128,2048]{1,0:T(8,128)(2,1)S(1)} %get-tuple-element.14), channel_id=1, source_target_pairs={{0,16},{1,17},{2,18},{3,19},{4,20},{5,21},{6,22},{7,23},{8,24},{9,... | collective-permute-start | bytes 1572872 | tf_op jit(solution)/shard_map/ppermute | solution.py:21
  69.7 9.5 %collective-permute-start.16 = (bf16[128,2048]{1,0:T(8,128)(2,1)S(1)}, bf16[128,2048]{1,0:T(8,128)(2,1)S(1)}, u32[]{:S(2)}, u32[]{:S(2)}) collective-permute-start(bf16[128,2048]{1,0:T(8,128)(2,1)S(1)} %slice.166), channel_id=1, source_target_pairs={{0,48},{1,49},{2,50},{3,51},{4,52},{5,53},{6,54},{7,55},{8,56},{9,... | collective-permute-start | bytes 1572872 | tf_op jit(solution)/shard_map/ppermute | solution.py:21
  73.9 10.9 %collective-permute-start.23 = (bf16[128,2048]{1,0:T(8,128)(2,1)S(1)}, bf16[128,2048]{1,0:T(8,128)(2,1)S(1)}, u32[]{:S(2)}, u32[]{:S(2)}) collective-permute-start(bf16[128,2048]{1,0:T(8,128)(2,1)S(1)} %get-tuple-element.15), channel_id=1, source_target_pairs={{0,48},{1,49},{2,50},{3,51},{4,52},{5,53},{6,54},{7,55},{8,56},{9,... | collective-permute-start | bytes 1572872 | tf_op jit(solution)/shard_map/ppermute | solution.py:21
  76.0 10.5 %collective-permute-start.15 = (bf16[128,2048]{1,0:T(8,128)(2,1)S(1)}, bf16[128,2048]{1,0:T(8,128)(2,1)S(1)}, u32[]{:S(2)}, u32[]{:S(2)}) collective-permute-start(bf16[128,2048]{1,0:T(8,128)(2,1)S(1)} %slice.163), channel_id=1, source_target_pairs={{0,16},{1,17},{2,18},{3,19},{4,20},{5,21},{6,22},{7,23},{8,24},{9,... | collective-permute-start | bytes 1572872 | tf_op jit(solution)/shard_map/ppermute | solution.py:21
  79.4 11.1 %collective-permute-start.17 = (bf16[128,2048]{1,0:T(8,128)(2,1)S(1)}, bf16[128,2048]{1,0:T(8,128)(2,1)S(1)}, u32[]{:S(2)}, u32[]{:S(2)}) collective-permute-start(bf16[128,2048]{1,0:T(8,128)(2,1)S(1)} %add_convert_fusion.1), channel_id=1, source_target_pairs={{0,48},{1,49},{2,50},{3,51},{4,52},{5,53},{6,54},{7,55},{8,56},{9,... | collective-permute-start | bytes 1572872 | tf_op jit(solution)/shard_map/ppermute | solution.py:21
  82.3 10.5 %collective-permute-start.22 = (bf16[128,2048]{1,0:T(8,128)(2,1)S(1)}, bf16[128,2048]{1,0:T(8,128)(2,1)S(1)}, u32[]{:S(2)}, u32[]{:S(2)}) collective-permute-start(bf16[128,2048]{1,0:T(8,128)(2,1)S(1)} %add_convert_fusion), channel_id=1, source_target_pairs={{0,16},{1,17},{2,18},{3,19},{4,20},{5,21},{6,22},{7,23},{8,24},{9,... | collective-permute-start | bytes 1572872 | tf_op jit(solution)/shard_map/ppermute | solution.py:21
  93.3 11.3 %collective-permute-start.18 = (bf16[64,2048]{1,0:T(8,128)(2,1)S(1)}, bf16[64,2048]{1,0:T(8,128)(2,1)S(1)}, u32[]{:S(2)}, u32[]{:S(2)}) collective-permute-start(bf16[64,2048]{1,0:T(8,128)(2,1)S(1)} %slice.210), channel_id=1, source_target_pairs={{0,4},{1,5},{2,6},{3,7},{4,8},{5,9},{6,10},{7,11},{8,12},{9,13},{1... | collective-permute-start | bytes 786440 | tf_op jit(solution)/shard_map/ppermute | solution.py:21
  93.4 11.5 %collective-permute-start.24 = (bf16[64,2048]{1,0:T(8,128)(2,1)S(1)}, bf16[64,2048]{1,0:T(8,128)(2,1)S(1)}, u32[]{:S(2)}, u32[]{:S(2)}) collective-permute-start(bf16[64,2048]{1,0:T(8,128)(2,1)S(1)} %get-tuple-element.16), channel_id=1, source_target_pairs={{0,8},{1,9},{2,10},{3,11},{4,12},{5,13},{6,14},{7,15},{8,0},{9,1},... | collective-permute-start | bytes 786440 | tf_op jit(solution)/shard_map/ppermute | solution.py:21
  105.1 10.8 %collective-permute-start.26 = (bf16[16,2048]{1,0:T(8,128)(2,1)S(1)}, bf16[16,2048]{1,0:T(8,128)(2,1)S(1)}, u32[]{:S(2)}, u32[]{:S(2)}) collective-permute-start(bf16[16,2048]{1,0:T(8,128)(2,1)S(1)} %get-tuple-element.18), channel_id=1, source_target_pairs={{0,1},{1,2},{2,3},{3,0},{4,5},{5,6},{6,7},{7,4},{8,9},{9,10},{10,1... | collective-permute-start | bytes 196616 | tf_op jit(solution)/shard_map/ppermute | solution.py:21
  106.9 8.9 %collective-permute-start.28 = (bf16[16,2048]{1,0:T(8,128)(2,1)S(1)}, bf16[16,2048]{1,0:T(8,128)(2,1)S(1)}, u32[]{:S(2)}, u32[]{:S(2)}) collective-permute-start(bf16[16,2048]{1,0:T(8,128)(2,1)S(1)} %get-tuple-element.19), channel_id=1, source_target_pairs={{0,3},{1,0},{2,1},{3,2},{4,7},{5,4},{6,5},{7,6},{8,11},{9,8},{10,9... | collective-permute-start | bytes 196616 | tf_op jit(solution)/shard_map/ppermute | solution.py:21
  (11 other events, 77.1 us)

commit v3 on v2

--- a/solution.py
+++ b/solution.py
@@ -6,8 +6,8 @@
 from jax.sharding import PartitionSpec as P
 
 STRIDE = {"x": 1, "y": 4, "z": 16}
-ORDER = (("x", "y", "z"), ("x", "z", "y"))
-SLAB_CUTS = (4, 4)
+ORDER = (("z", "x", "y"), ("z", "y", "x"))
+SLAB_CUTS = (5, 3)
 
 
 def hop(value, phase, offset):
@@ -38,10 +38,12 @@
     core = lax.axis_index("row")
     ks = lax.broadcasted_iota(jnp.int32, (64,), 0)
     k3, k2, k1 = ks // 16, (ks // 4) % 4, ks % 4
-    dz = jnp.where(core == 0, k3, k2)
-    dy = jnp.where(core == 0, k2, k3)
-    z, y, x = chip // 16, (chip // 4) % 4, chip % 4
-    return ((z + dz) % 4) * 16 + ((y + dy) % 4) * 4 + (x + k1) % 4
+    block = 0
+    for axis, stride in STRIDE.items():
+        first, second = (dict(zip(axes, (k1, k2, k3)))[axis] for axes in ORDER)
+        at = (chip // stride) % 4
+        block = block + ((at + jnp.where(core == 0, first, second)) % 4) * stride
+    return block
 
 
 def place(k3, k2):
@@ -213,17 +215,20 @@
         slab_grad = slab_product(pieces, early, late, slab_grad, first, count)
         first += count
 
-    total = jnp.concatenate(
-        [
-            back0[:half] + top_from1.astype(jnp.float32) + top_from3.astype(jnp.float32),
-            back0[half:] + low_from1.astype(jnp.float32) + low_from3.astype(jnp.float32),
-        ]
-    )
-    for phase in (1, 0):
-        cut = total.reshape(4, -1, total.shape[-1])
-        total = cut[0]
-        for k in (1, 2, 3):
-            total = total + hop(cut[k].astype(jnp.bfloat16), phase, k).astype(jnp.float32)
+    upper = back0[:half] + top_from1.astype(jnp.float32) + top_from3.astype(jnp.float32)
+    mid = half // 2
+    piece = upper[mid:].astype(jnp.bfloat16)
+    own_part, piece, low0 = lax.optimization_barrier((upper[:mid], piece, back0[half:]))
+    folded = hop(piece, 1, 1)
+    lower = low0 + low_from1.astype(jnp.float32) + low_from3.astype(jnp.float32)
+    total = own_part + folded.astype(jnp.float32)
+    for k in (2, 3):
+        piece = lower[(k - 2) * mid : (k - 1) * mid].astype(jnp.bfloat16)
+        total = total + hop(piece, 1, k).astype(jnp.float32)
+    cut = total.reshape(4, -1, total.shape[-1])
+    total = cut[0]
+    for k in (1, 2, 3):
+        total = total + hop(cut[k].astype(jnp.bfloat16), 0, k).astype(jnp.float32)
     return total, slab_grad
 
 

time: 117 us -> 124 us (1.060)
  waiting for transfers between devices: 31.6 us -> 40 us
  starting transfers between devices: 40.4 us -> 38.7 us
    ppermute x24, waiting for transfers between devices: 31.6 us -> 40 us  [hop(): return lax.ppermute(value, ('row', 'col'), pairs)]
    ppermute x24, starting transfers between devices: 39.9 us -> 38.3 us  [hop(): return lax.ppermute(value, ('row', 'col'), pairs)]
  transfers between devices with their start and end apart: 29 -> 29, of which waited for: 11 -> 10; matrix products, arithmetic and copies ran while one was open for 21% -> 20% of each run, Pallas kernels for 14% -> 13%
where the time goes in v3:
time: 124 us; the launch traced here: 123 us
  waiting for transfers between devices  40 us (32%)
  starting transfers between devices  38.7 us (31%)
  matrix products  20.4 us (16%)
  Pallas kernels  16.4 us (13%)
  local copies, waits for them, and re-layouts  4.57 us (4%)
  other arithmetic  2.27 us (2%)
    ppermute x24, waiting for transfers between devices, hop(): return lax.ppermute(value, ('row', 'col'), pairs)  40 us
    ppermute x24, starting transfers between devices, hop(): return lax.ppermute(value, ('row', 'col'), pairs)  38.3 us
    pallas_call x2, Pallas kernels, slab_product(): pl.pallas_call(lambda *refs: slab_kernel(len(pieces), *refs), grid=(count...  13.6 us
    dot_general x5, matrix products, body(): part = jnp.dot(rows, slab_weight, preferred_element_type=jnp.float32)  9.68 us
    dot_general x4, matrix products, times_transpose(): lax.dot_general(rows, slab_weight, (((1,), (1,)), ((), ())), preferred_el...  9.44 us
  transfers between devices with their start and end apart: 29, of which 10 were waited for; matrix products, arithmetic and copies ran while one was open for 20% of the time, Pallas kernels for 13%

profile of v3, /device:TPU:0, one launch (start us, length us, event | category | flops | bytes accessed | tf_op | source)
XLA Modules:
  0.0 123.4 jit_solution(15726800562633653713)
XLA Ops:
  0.6 4.2 %collective-permute-start = (bf16[16,2048]{1,0:T(8,128)(2,1)}, bf16[16,2048]{1,0:T(8,128)(2,1)S(1)}, u32[]{:S(2)}, u32[]{:S(2)}) collective-permute-start(bf16[16,2048]{1,0:T(8,128)(2,1)} %source_ref.2), channel_id=1, source_target_pairs={{0,48},{1,49},{2,50},{3,51},{4,52},{5,53},{6,54},{7,55},{8,56},{9,... | collective-permute-start | bytes 196616 | tf_op jit(solution)/shard_map/ppermute | solution.py:21
  12.7 2.8 %collective-permute-start.3 = (bf16[64,2048]{1,0:T(8,128)(2,1)S(1)}, bf16[64,2048]{1,0:T(8,128)(2,1)S(1)}, u32[]{:S(2)}, u32[]{:S(2)}) collective-permute-start(bf16[64,2048]{1,0:T(8,128)(2,1)S(1)} %bitcast.45), channel_id=1, source_target_pairs={{0,3},{1,0},{2,1},{3,2},{4,7},{5,4},{6,5},{7,6},{8,11},{9,8},{10,9... | collective-permute-start | bytes 786440 | tf_op jit(solution)/shard_map/ppermute | solution.py:21
  15.6 2.3 %collective-permute-start.4 = (bf16[64,2048]{1,0:T(8,128)(2,1)S(1)}, bf16[64,2048]{1,0:T(8,128)(2,1)S(1)}, u32[]{:S(2)}, u32[]{:S(2)}) collective-permute-start(bf16[64,2048]{1,0:T(8,128)(2,1)S(1)} %bitcast.47), channel_id=1, source_target_pairs={{0,2},{1,3},{2,0},{3,1},{4,6},{5,7},{6,4},{7,5},{8,10},{9,11},{10,... | collective-permute-start | bytes 786440 | tf_op jit(solution)/shard_map/ppermute | solution.py:21
  19.4 6.5 %collective-permute-done.5 = bf16[64,2048]{1,0:T(8,128)(2,1)S(1)} collective-permute-done((bf16[64,2048]{1,0:T(8,128)(2,1)S(1)}, bf16[64,2048]{1,0:T(8,128)(2,1)S(1)}, u32[]{:S(2)}, u32[]{:S(2)}) %collective-permute-start.5) | collective-permute-done | bytes 262176 | tf_op jit(solution)/shard_map/ppermute | solution.py:21
  26.2 2.5 %collective-permute-start.9 = (bf16[128,2048]{1,0:T(8,128)(2,1)S(1)}, bf16[128,2048]{1,0:T(8,128)(2,1)S(1)}, u32[]{:S(2)}, u32[]{:S(2)}) collective-permute-start(bf16[128,2048]{1,0:T(8,128)(2,1)S(1)} %bitcast.58), channel_id=1, source_target_pairs={{0,4},{1,5},{2,6},{3,7},{4,8},{5,9},{6,10},{7,11},{8,12},{9,13},{1... | collective-permute-start | bytes 1572872 | tf_op jit(solution)/shard_map/ppermute | solution.py:21
  30.7 2.5 %collective-permute-start.6 = (bf16[128,2048]{1,0:T(8,128)(2,1)S(1)}, bf16[128,2048]{1,0:T(8,128)(2,1)S(1)}, u32[]{:S(2)}, u32[]{:S(2)}) collective-permute-start(bf16[128,2048]{1,0:T(8,128)(2,1)S(1)} %bitcast.61), channel_id=1, source_target_pairs={{0,12},{1,13},{2,14},{3,15},{4,0},{5,1},{6,2},{7,3},{8,4},{9,5},{1... | collective-permute-start | bytes 1572872 | tf_op jit(solution)/shard_map/ppermute | solution.py:21
  33.2 2.4 %fusion.3.refs_0_ = bf16[256,2048]{1,0:T(8,128)(2,1)S(1)} fusion(bf16[256,2048]{1,0:T(8,128)(2,1)S(1)} %bitcast.37, bf16[2048,2048]{1,0:T(8,128)(2,1)S(1)} %bring_in.3, bf16[1024,2048]{1,0:T(8,128)(2,1)S(1)} %convolution_convert_fusion, f32[256]{0:T(256)S(1)} %slice-done), kind=kOutput, calls=%fused_computation.9 | convolution fusion | flops 2150105088 | bytes 11535360 | tf_op jit(solution)/shard_map/dot_general | solution.py:195
  35.6 7.0 %collective-permute-done.7.refs_1_ = bf16[128,2048]{1,0:T(8,128)(2,1)S(1)} collective-permute-done((bf16[128,2048]{1,0:T(8,128)(2,1)S(1)}, bf16[128,2048]{1,0:T(8,128)(2,1)S(1)}, u32[]{:S(2)}, u32[]{:S(2)}) %collective-permute-start.7) | collective-permute-done | bytes 524320 | tf_op jit(solution)/shard_map/ppermute | solution.py:21
  43.6 2.4 %fusion.4.refs_1_ = bf16[256,2048]{1,0:T(8,128)(2,1)S(1)} fusion(bf16[256,2048]{1,0:T(8,128)(2,1)S(1)} %bitcast.51, bf16[2048,2048]{1,0:T(8,128)(2,1)S(1)} %bring_in.3, bf16[128,2048]{1,0:T(8,128)(2,1)S(1)} %get-tuple-element.17, bf16[128,2048]{1,0:T(8,128)(2,1)S(1)} %get-tuple-element.14, f32[256]{0:T(256)S(1)} %pad_maximum_fusion.6), kind=kOutput, calls=%fused_computation.10 | convolution fusion | flops 2151677952 | bytes 11535360 | tf_op jit(solution)/shard_map/dot_general | solution.py:195
  47.6 2.4 %fusion.5.refs_2_.refs_0_ = bf16[256,2048]{1,0:T(8,128)(2,1)S(1)} fusion(bf16[256,2048]{1,0:T(8,128)(2,1)S(1)} %bitcast.50, bf16[2048,2048]{1,0:T(8,128)(2,1)S(1)} %bring_in.3, bf16[128,2048]{1,0:T(8,128)(2,1)S(1)} %get-tuple-element.15, bf16[128,2048]{1,0:T(8,128)(2,1)S(1)} %get-tuple-element.16, f32[256]{0:T(256)S(1)} %pad_maximum_fusion.7), kind=kOutput, calls=%fused_computation.11 | convolution fusion | flops 2151677952 | bytes 11535360 | tf_op jit(solution)/shard_map/dot_general | solution.py:195
  50.0 2.1 %collective-permute-start.10 = (bf16[128,2048]{1,0:T(8,128)(2,1)S(1)}, bf16[128,2048]{1,0:T(8,128)(2,1)S(1)}, u32[]{:S(2)}, u32[]{:S(2)}) collective-permute-start(bf16[128,2048]{1,0:T(8,128)(2,1)S(1)} %collective-permute-done.6.refs_2_), channel_id=1, source_target_pairs={{0,12},{1,13},{2,14},{3,15},{4,0},{5,1},{6,2},{7,3},{8,4},{9,5},{1... | collective-permute-start | bytes 1572872 | tf_op jit(solution)/shard_map/ppermute | solution.py:21
  52.2 4.6 %collective-permute-done.19.refs_5_ = bf16[128,2048]{1,0:T(8,128)(2,1)S(1)} collective-permute-done((bf16[128,2048]{1,0:T(8,128)(2,1)S(1)}, bf16[128,2048]{1,0:T(8,128)(2,1)S(1)}, u32[]{:S(2)}, u32[]{:S(2)}) %collective-permute-start.19) | collective-permute-done | bytes 524320 | tf_op jit(solution)/shard_map/ppermute | solution.py:21
  61.3 2.4 %convolution_convert_fusion.1 = bf16[256,2048]{1,0:T(8,128)(2,1)S(1)} fusion(bf16[256,2048]{1,0:T(8,128)(2,1)S(1)} %residual.3.refs_8_, bf16[2048,2048]{1,0:T(8,128)(2,1)S(1)} %bring_in.3), kind=kOutput, calls=%fused_computation.12 | convolution fusion | flops 2148007936 | bytes 10485760 | tf_op jit(solution)/shard_map/dot_general | solution.py:156
  66.9 2.4 %convolution_convert_fusion.2 = bf16[256,2048]{1,0:T(8,128)(2,1)S(1)} fusion(bf16[2048,2048]{1,0:T(8,128)(2,1)S(1)} %bring_in.3, bf16[768,2048]{1,0:T(8,128)(2,1)S(1)} %residual.2.refs_7_), kind=kOutput, calls=%fused_computation.13 | convolution fusion | flops 2148007936 | bytes 10485760 | tf_op jit(solution)/shard_map/dot_general | solution.py:156
  69.3 2.2 %collective-permute-start.16 = (bf16[128,2048]{1,0:T(8,128)(2,1)S(1)}, bf16[128,2048]{1,0:T(8,128)(2,1)S(1)}, u32[]{:S(2)}, u32[]{:S(2)}) collective-permute-start(bf16[128,2048]{1,0:T(8,128)(2,1)S(1)} %slice.158), channel_id=1, source_target_pairs={{0,12},{1,13},{2,14},{3,15},{4,0},{5,1},{6,2},{7,3},{8,4},{9,5},{1... | collective-permute-start | bytes 1572872 | tf_op jit(solution)/shard_map/ppermute | solution.py:21
  71.5 2.4 %convolution_convert_fusion.3 = bf16[256,2048]{1,0:T(8,128)(2,1)S(1)} fusion(bf16[2048,2048]{1,0:T(8,128)(2,1)S(1)} %bring_in.3, bf16[768,2048]{1,0:T(8,128)(2,1)S(1)} %residual.2.refs_7_), kind=kOutput, calls=%fused_computation.14 | convolution fusion | flops 2148007936 | bytes 10485760 | tf_op jit(solution)/shard_map/dot_general | solution.py:156
  74.1 4.7 %collective-permute-done.16 = bf16[128,2048]{1,0:T(8,128)(2,1)S(1)} collective-permute-done((bf16[128,2048]{1,0:T(8,128)(2,1)S(1)}, bf16[128,2048]{1,0:T(8,128)(2,1)S(1)}, u32[]{:S(2)}, u32[]{:S(2)}) %collective-permute-start.16) | collective-permute-done | bytes 524320 | tf_op jit(solution)/shard_map/ppermute | solution.py:21
  78.9 3.2 %collective-permute-start.17 = (bf16[128,2048]{1,0:T(8,128)(2,1)S(1)}, bf16[128,2048]{1,0:T(8,128)(2,1)S(1)}, u32[]{:S(2)}, u32[]{:S(2)}) collective-permute-start(bf16[128,2048]{1,0:T(8,128)(2,1)S(1)} %add_convert_fusion.2), channel_id=1, source_target_pairs={{0,12},{1,13},{2,14},{3,15},{4,0},{5,1},{6,2},{7,3},{8,4},{9,5},{1... | collective-permute-start | bytes 1572872 | tf_op jit(solution)/shard_map/ppermute | solution.py:21
  82.1 2.4 %fusion.13 = f32[256,2048]{1,0:T(8,128)S(1)} fusion(bf16[2048,2048]{1,0:T(8,128)(2,1)S(1)} %bring_in.3, bf16[768,2048]{1,0:T(8,128)(2,1)S(1)} %residual.2.refs_7_), kind=kOutput, calls=%fused_computation.25 | convolution fusion | flops 2147483648 | bytes 11534336 | tf_op jit(solution)/shard_map/dot_general | solution.py:156
  89.2 5.2 %collective-permute-done.23 = bf16[128,2048]{1,0:T(8,128)(2,1)S(1)} collective-permute-done((bf16[128,2048]{1,0:T(8,128)(2,1)S(1)}, bf16[128,2048]{1,0:T(8,128)(2,1)S(1)}, u32[]{:S(2)}, u32[]{:S(2)}) %collective-permute-start.23) | collective-permute-done | bytes 524320 | tf_op jit(solution)/shard_map/ppermute | solution.py:21
  94.4 7.1 %collective-permute-done.22 = bf16[128,2048]{1,0:T(8,128)(2,1)S(1)} collective-permute-done((bf16[128,2048]{1,0:T(8,128)(2,1)S(1)}, bf16[128,2048]{1,0:T(8,128)(2,1)S(1)}, u32[]{:S(2)}, u32[]{:S(2)}) %collective-permute-start.22) | collective-permute-done | bytes 524320 | tf_op jit(solution)/shard_map/ppermute | solution.py:21
  104.5 8.1 %slab_grad.2.refs_9_ = f32[2048,2048]{1,0:T(8,128)} custom-call(bf16[128,2048]{1,0:T(8,128)(2,1)S(1)} %collective-permute-done.10.refs_0_, bf16[128,2048]{1,0:T(8,128)(2,1)S(1)} %collective-permute-done.7.refs_1_, bf16[128,2048]{1,0:T(8,128)(2,1)S(1)} %collective-permute-done.6.refs_2_, bf16[128,2048]{1,0:T(8,128)(2,1)S(1)} %collective-permute-done.8.refs_3_, ...), custom_call_target="tpu_custom_call" | custom-call | flops 5368709120 | bytes 17301504 | tf_op jit(solution)/shard_map/slab_grad/pallas_call | solution.py:115
  112.9 2.3 %collective-permute-start.26 = (bf16[16,2048]{1,0:T(8,128)(2,1)S(1)}, bf16[16,2048]{1,0:T(8,128)(2,1)S(1)}, u32[]{:S(2)}, u32[]{:S(2)}) collective-permute-start(bf16[16,2048]{1,0:T(8,128)(2,1)S(1)} %get-tuple-element.24), channel_id=1, source_target_pairs={{0,16},{1,17},{2,18},{3,19},{4,20},{5,21},{6,22},{7,23},{8,24},{9,... | collective-permute-start | bytes 196616 | tf_op jit(solution)/shard_map/ppermute | solution.py:21
  117.3 5.4 %slab_grad.3 = f32[2048,2048]{1,0:T(8,128)} custom-call(bf16[128,2048]{1,0:T(8,128)(2,1)S(1)} %collective-permute-done.10.refs_0_, bf16[128,2048]{1,0:T(8,128)(2,1)S(1)} %collective-permute-done.7.refs_1_, bf16[128,2048]{1,0:T(8,128)(2,1)S(1)} %collective-permute-done.6.refs_2_, ...), custom_call_target="tpu_custom_call", output_to_operand_aliasing={{}: (9, {})} | custom-call | flops 3221225472 | bytes 12058624 | tf_op jit(solution)/shard_map/slab_grad/pallas_call | solution.py:115
  (94 shorter events, 33.1 us)
Async XLA Ops:
  0.6 11.9 %collective-permute-start = (bf16[16,2048]{1,0:T(8,128)(2,1)}, bf16[16,2048]{1,0:T(8,128)(2,1)S(1)}, u32[]{:S(2)}, u32[]{:S(2)}) collective-permute-start(bf16[16,2048]{1,0:T(8,128)(2,1)} %source_ref.2), channel_id=1, source_target_pairs={{0,48},{1,49},{2,50},{3,51},{4,52},{5,53},{6,54},{7,55},{8,56},{9,... | collective-permute-start | bytes 196616 | tf_op jit(solution)/shard_map/ppermute | solution.py:21
  4.9 7.7 %collective-permute-start.2 = (bf16[16,2048]{1,0:T(8,128)(2,1)}, bf16[16,2048]{1,0:T(8,128)(2,1)S(1)}, u32[]{:S(2)}, u32[]{:S(2)}) collective-permute-start(bf16[16,2048]{1,0:T(8,128)(2,1)} %source_ref.2), channel_id=1, source_target_pairs={{0,16},{1,17},{2,18},{3,19},{4,20},{5,21},{6,22},{7,23},{8,24},{9,... | collective-permute-start | bytes 196616 | tf_op jit(solution)/shard_map/ppermute | solution.py:21
  4.9 7.7 %collective-permute-start.1 = (bf16[16,2048]{1,0:T(8,128)(2,1)}, bf16[16,2048]{1,0:T(8,128)(2,1)S(1)}, u32[]{:S(2)}, u32[]{:S(2)}) collective-permute-start(bf16[16,2048]{1,0:T(8,128)(2,1)} %source_ref.2), channel_id=1, source_target_pairs={{0,32},{1,33},{2,34},{3,35},{4,36},{5,37},{6,38},{7,39},{8,40},{9,... | collective-permute-start | bytes 196616 | tf_op jit(solution)/shard_map/ppermute | solution.py:21
  15.5 10.5 %collective-permute-start.5 = (bf16[64,2048]{1,0:T(8,128)(2,1)S(1)}, bf16[64,2048]{1,0:T(8,128)(2,1)S(1)}, u32[]{:S(2)}, u32[]{:S(2)}) collective-permute-start(bf16[64,2048]{1,0:T(8,128)(2,1)S(1)} %bitcast.46), channel_id=1, source_target_pairs={{0,1},{1,2},{2,3},{3,0},{4,5},{5,6},{6,7},{7,4},{8,9},{9,10},{10,1... | collective-permute-start | bytes 786440 | tf_op jit(solution)/shard_map/ppermute | solution.py:21
  15.6 10.4 %collective-permute-start.4 = (bf16[64,2048]{1,0:T(8,128)(2,1)S(1)}, bf16[64,2048]{1,0:T(8,128)(2,1)S(1)}, u32[]{:S(2)}, u32[]{:S(2)}) collective-permute-start(bf16[64,2048]{1,0:T(8,128)(2,1)S(1)} %bitcast.47), channel_id=1, source_target_pairs={{0,2},{1,3},{2,0},{3,1},{4,6},{5,7},{6,4},{7,5},{8,10},{9,11},{10,... | collective-permute-start | bytes 786440 | tf_op jit(solution)/shard_map/ppermute | solution.py:21
  26.2 19.8 %collective-permute-start.9 = (bf16[128,2048]{1,0:T(8,128)(2,1)S(1)}, bf16[128,2048]{1,0:T(8,128)(2,1)S(1)}, u32[]{:S(2)}, u32[]{:S(2)}) collective-permute-start(bf16[128,2048]{1,0:T(8,128)(2,1)S(1)} %bitcast.58), channel_id=1, source_target_pairs={{0,4},{1,5},{2,6},{3,7},{4,8},{5,9},{6,10},{7,11},{8,12},{9,13},{1... | collective-permute-start | bytes 1572872 | tf_op jit(solution)/shard_map/ppermute | solution.py:21
  28.7 17.4 %collective-permute-start.8 = (bf16[128,2048]{1,0:T(8,128)(2,1)S(1)}, bf16[128,2048]{1,0:T(8,128)(2,1)S(1)}, u32[]{:S(2)}, u32[]{:S(2)}) collective-permute-start(bf16[128,2048]{1,0:T(8,128)(2,1)S(1)} %bitcast.59), channel_id=1, source_target_pairs={{0,12},{1,13},{2,14},{3,15},{4,0},{5,1},{6,2},{7,3},{8,4},{9,5},{1... | collective-permute-start | bytes 1572872 | tf_op jit(solution)/shard_map/ppermute | solution.py:21
  29.9 12.7 %collective-permute-start.7 = (bf16[128,2048]{1,0:T(8,128)(2,1)S(1)}, bf16[128,2048]{1,0:T(8,128)(2,1)S(1)}, u32[]{:S(2)}, u32[]{:S(2)}) collective-permute-start(bf16[128,2048]{1,0:T(8,128)(2,1)S(1)} %bitcast.60), channel_id=1, source_target_pairs={{0,4},{1,5},{2,6},{3,7},{4,8},{5,9},{6,10},{7,11},{8,12},{9,13},{1... | collective-permute-start | bytes 1572872 | tf_op jit(solution)/shard_map/ppermute | solution.py:21
  30.7 12.8 %collective-permute-start.6 = (bf16[128,2048]{1,0:T(8,128)(2,1)S(1)}, bf16[128,2048]{1,0:T(8,128)(2,1)S(1)}, u32[]{:S(2)}, u32[]{:S(2)}) collective-permute-start(bf16[128,2048]{1,0:T(8,128)(2,1)S(1)} %bitcast.61), channel_id=1, source_target_pairs={{0,12},{1,13},{2,14},{3,15},{4,0},{5,1},{6,2},{7,3},{8,4},{9,5},{1... | collective-permute-start | bytes 1572872 | tf_op jit(solution)/shard_map/ppermute | solution.py:21
  35.5 29.8 %collective-permute-start.11 = (bf16[256,2048]{1,0:T(8,128)(2,1)S(1)}, bf16[256,2048]{1,0:T(8,128)(2,1)S(1)}, u32[]{:S(2)}, u32[]{:S(2)}) collective-permute-start(bf16[256,2048]{1,0:T(8,128)(2,1)S(1)} %fusion.3.refs_0_), channel_id=1, source_target_pairs={{0,64},{64,0},{1,65},{65,1},{2,66},{66,2},{3,67},{67,3},{4,68},{68... | collective-permute-start | bytes 3145736 | tf_op jit(solution)/shard_map/ppermute | solution.py:29
  45.9 19.4 %collective-permute-start.12 = (bf16[256,2048]{1,0:T(8,128)(2,1)S(1)}, bf16[256,2048]{1,0:T(8,128)(2,1)S(1)}, u32[]{:S(2)}, u32[]{:S(2)}) collective-permute-start(bf16[256,2048]{1,0:T(8,128)(2,1)S(1)} %fusion.4.refs_1_), channel_id=1, source_target_pairs={{0,64},{64,0},{1,65},{65,1},{2,66},{66,2},{3,67},{67,3},{4,68},{68... | collective-permute-start | bytes 3145736 | tf_op jit(solution)/shard_map/ppermute | solution.py:29
  46.1 10.6 %collective-permute-start.19 = (bf16[128,2048]{1,0:T(8,128)(2,1)S(1)}, bf16[128,2048]{1,0:T(8,128)(2,1)S(1)}, u32[]{:S(2)}, u32[]{:S(2)}) collective-permute-start(bf16[128,2048]{1,0:T(8,128)(2,1)S(1)} %collective-permute-done.9.refs_6_), channel_id=1, source_target_pairs={{0,4},{1,5},{2,6},{3,7},{4,8},{5,9},{6,10},{7,11},{8,12},{9,13},{1... | collective-permute-start | bytes 1572872 | tf_op jit(solution)/shard_map/ppermute | solution.py:21
  49.9 10.8 %collective-permute-start.13 = (bf16[256,2048]{1,0:T(8,128)(2,1)S(1)}, bf16[256,2048]{1,0:T(8,128)(2,1)S(1)}, u32[]{:S(2)}, u32[]{:S(2)}) collective-permute-start(bf16[256,2048]{1,0:T(8,128)(2,1)S(1)} %fusion.5.refs_2_.refs_0_), channel_id=1, source_target_pairs={{0,64},{64,0},{1,65},{65,1},{2,66},{66,2},{3,67},{67,3},{4,68},{68... | collective-permute-start | bytes 3145736 | tf_op jit(solution)/shard_map/ppermute | solution.py:29
  50.0 9.2 %collective-permute-start.10 = (bf16[128,2048]{1,0:T(8,128)(2,1)S(1)}, bf16[128,2048]{1,0:T(8,128)(2,1)S(1)}, u32[]{:S(2)}, u32[]{:S(2)}) collective-permute-start(bf16[128,2048]{1,0:T(8,128)(2,1)S(1)} %collective-permute-done.6.refs_2_), channel_id=1, source_target_pairs={{0,12},{1,13},{2,14},{3,15},{4,0},{5,1},{6,2},{7,3},{8,4},{9,5},{1... | collective-permute-start | bytes 1572872 | tf_op jit(solution)/shard_map/ppermute | solution.py:21
  63.8 21.5 %collective-permute-start.21 = (bf16[128,2048]{1,0:T(8,128)(2,1)S(1)}, bf16[128,2048]{1,0:T(8,128)(2,1)S(1)}, u32[]{:S(2)}, u32[]{:S(2)}) collective-permute-start(bf16[128,2048]{1,0:T(8,128)(2,1)S(1)} %get-tuple-element.20), channel_id=1, source_target_pairs={{0,4},{1,5},{2,6},{3,7},{4,8},{5,9},{6,10},{7,11},{8,12},{9,13},{1... | collective-permute-start | bytes 1572872 | tf_op jit(solution)/shard_map/ppermute | solution.py:21
  69.3 9.5 %collective-permute-start.16 = (bf16[128,2048]{1,0:T(8,128)(2,1)S(1)}, bf16[128,2048]{1,0:T(8,128)(2,1)S(1)}, u32[]{:S(2)}, u32[]{:S(2)}) collective-permute-start(bf16[128,2048]{1,0:T(8,128)(2,1)S(1)} %slice.158), channel_id=1, source_target_pairs={{0,12},{1,13},{2,14},{3,15},{4,0},{5,1},{6,2},{7,3},{8,4},{9,5},{1... | collective-permute-start | bytes 1572872 | tf_op jit(solution)/shard_map/ppermute | solution.py:21
  73.9 12.8 %collective-permute-start.15 = (bf16[128,2048]{1,0:T(8,128)(2,1)S(1)}, bf16[128,2048]{1,0:T(8,128)(2,1)S(1)}, u32[]{:S(2)}, u32[]{:S(2)}) collective-permute-start(bf16[128,2048]{1,0:T(8,128)(2,1)S(1)} %slice.155), channel_id=1, source_target_pairs={{0,4},{1,5},{2,6},{3,7},{4,8},{5,9},{6,10},{7,11},{8,12},{9,13},{1... | collective-permute-start | bytes 1572872 | tf_op jit(solution)/shard_map/ppermute | solution.py:21
  78.9 9.9 %collective-permute-start.17 = (bf16[128,2048]{1,0:T(8,128)(2,1)S(1)}, bf16[128,2048]{1,0:T(8,128)(2,1)S(1)}, u32[]{:S(2)}, u32[]{:S(2)}) collective-permute-start(bf16[128,2048]{1,0:T(8,128)(2,1)S(1)} %add_convert_fusion.2), channel_id=1, source_target_pairs={{0,12},{1,13},{2,14},{3,15},{4,0},{5,1},{6,2},{7,3},{8,4},{9,5},{1... | collective-permute-start | bytes 1572872 | tf_op jit(solution)/shard_map/ppermute | solution.py:21
  84.5 10.0 %collective-permute-start.23 = (bf16[128,2048]{1,0:T(8,128)(2,1)S(1)}, bf16[128,2048]{1,0:T(8,128)(2,1)S(1)}, u32[]{:S(2)}, u32[]{:S(2)}) collective-permute-start(bf16[128,2048]{1,0:T(8,128)(2,1)S(1)} %get-tuple-element.21), channel_id=1, source_target_pairs={{0,12},{1,13},{2,14},{3,15},{4,0},{5,1},{6,2},{7,3},{8,4},{9,5},{1... | collective-permute-start | bytes 1572872 | tf_op jit(solution)/shard_map/ppermute | solution.py:21
  85.4 16.1 %collective-permute-start.22 = (bf16[128,2048]{1,0:T(8,128)(2,1)S(1)}, bf16[128,2048]{1,0:T(8,128)(2,1)S(1)}, u32[]{:S(2)}, u32[]{:S(2)}) collective-permute-start(bf16[128,2048]{1,0:T(8,128)(2,1)S(1)} %add_convert_fusion.1), channel_id=1, source_target_pairs={{0,4},{1,5},{2,6},{3,7},{4,8},{5,9},{6,10},{7,11},{8,12},{9,13},{1... | collective-permute-start | bytes 1572872 | tf_op jit(solution)/shard_map/ppermute | solution.py:21
  89.1 23.5 %collective-permute-start.18 = (bf16[64,2048]{1,0:T(8,128)(2,1)S(1)}, bf16[64,2048]{1,0:T(8,128)(2,1)S(1)}, u32[]{:S(2)}, u32[]{:S(2)}) collective-permute-start(bf16[64,2048]{1,0:T(8,128)(2,1)S(1)} %slice.192), channel_id=1, source_target_pairs={{0,1},{1,2},{2,3},{3,0},{4,5},{5,6},{6,7},{7,4},{8,9},{9,10},{10,1... | collective-permute-start | bytes 786440 | tf_op jit(solution)/shard_map/ppermute | solution.py:21
  101.8 10.9 %collective-permute-start.24 = (bf16[64,2048]{1,0:T(8,128)(2,1)S(1)}, bf16[64,2048]{1,0:T(8,128)(2,1)S(1)}, u32[]{:S(2)}, u32[]{:S(2)}) collective-permute-start(bf16[64,2048]{1,0:T(8,128)(2,1)S(1)} %get-tuple-element.22), channel_id=1, source_target_pairs={{0,2},{1,3},{2,0},{3,1},{4,6},{5,7},{6,4},{7,5},{8,10},{9,11},{10,... | collective-permute-start | bytes 786440 | tf_op jit(solution)/shard_map/ppermute | solution.py:21
  103.0 9.7 %collective-permute-start.25 = (bf16[64,2048]{1,0:T(8,128)(2,1)S(1)}, bf16[64,2048]{1,0:T(8,128)(2,1)S(1)}, u32[]{:S(2)}, u32[]{:S(2)}) collective-permute-start(bf16[64,2048]{1,0:T(8,128)(2,1)S(1)} %get-tuple-element.23), channel_id=1, source_target_pairs={{0,3},{1,0},{2,1},{3,2},{4,7},{5,4},{6,5},{7,6},{8,11},{9,8},{10,9... | collective-permute-start | bytes 786440 | tf_op jit(solution)/shard_map/ppermute | solution.py:21
  112.9 9.9 %collective-permute-start.26 = (bf16[16,2048]{1,0:T(8,128)(2,1)S(1)}, bf16[16,2048]{1,0:T(8,128)(2,1)S(1)}, u32[]{:S(2)}, u32[]{:S(2)}) collective-permute-start(bf16[16,2048]{1,0:T(8,128)(2,1)S(1)} %get-tuple-element.24), channel_id=1, source_target_pairs={{0,16},{1,17},{2,18},{3,19},{4,20},{5,21},{6,22},{7,23},{8,24},{9,... | collective-permute-start | bytes 196616 | tf_op jit(solution)/shard_map/ppermute | solution.py:21
  (11 other events, 73.4 us)
